TPU v7x, 32 devices: a whole 2x2x4 slice. The times are simulated.
32 devices in a mesh: dp: 8 (over z, x), col: 4 (over y, core).
Axes of the slice: x: 2, y: 2, z: 4, core: 2. Of those that a mesh axis runs over, the one named last changes fastest.
Arguments:
- activations: bfloat16 [2, 7168, 8192], P(None, 'dp', 'col'), may hold values from -40 to 40
- cotangent: bfloat16 [2, 7168, 2048], P(None, 'dp'), may hold values from -40 to 40
- master_weights: float32 [2, 2048, 8192], P(None, 'dp', 'col'), may hold values from -6 to 6
- moment_codes: bfloat16 [2, 2048, 8192], P(None, 'dp', 'col'), may hold values from -1 to 1
- square_codes: bfloat16 [2, 2048, 8192], P(None, 'dp', 'col'), may hold values from 0.049804688 to 1
- moment_scales: float32 [2, 2048, 4], P(None, 'dp'), may hold values from 0.05 to 0.5
- square_scales: float32 [2, 2048, 4], P(None, 'dp'), may hold values from 0.005 to 0.05
Outputs:
- new_weights: float32 [2, 2048, 8192], P(None, 'dp', 'col')
- new_moment_codes: bfloat16 [2, 2048, 8192], P(None, 'dp', 'col')
- new_square_codes: bfloat16 [2, 2048, 8192], P(None, 'dp', 'col')
- new_moment_scales: float32 [2, 2048, 4], P(None, 'dp')
- new_square_scales: float32 [2, 2048, 4], P(None, 'dp')
All inputs are finite; a program needn't handle non-finite values. Where the computation divides by a largest or mean magnitude, that divisor is 1e-20 or more.
Results may differ from a plain program's by a relative error of at most 0.001.
Values sent between devices are 32-bit elements; how exact they have to be, the bound alone decides.
A program may use at most 128 MiB of HBM per device.

v0:
```python
import functools

import jax
import jax.numpy as jnp
from jax import lax
from jax.experimental import pallas as pl
from jax.experimental.pallas import tpu as pltpu
from jax.sharding import PartitionSpec as P

D = 8192
KV = 2048
BLOCK = 2048
LAYERS = 2
STEP = 10


beta_one = 0.9
beta_two = 0.999
learn_rate = 0.001
decay_rate = 0.1
adam_eps = 1e-08
scale_eps = 1e-06
norm_eps = 1e-06

LANES = 128
AHEAD = 3
XSLOTS = 4


def reduce_kernel(
    count, col_count, cot_ref, act_ref, out_ref, sq_ref,
    xs, xr, part, arr, bs, br, own_sq, sum_sq, col_sq, dp_sq,
    xs_sem, xr_sem, rs_sem, rr_sem, ls_sem, ll_sem, bs_sem, br_sem,
    cs_sem, cr_sem, ds_sem, dr_sem, x_free, from_right, from_left,
):
    layers, pairs, line, rows, tokens = cot_ref.shape
    cols = act_ref.shape[2]
    slots = part.shape[0]
    wide_per = cols // (2 * LANES) - 1
    per_layer = wide_per + 2
    period = (per_layer + 1) // 2
    items = layers * per_layer
    wides = layers * wide_per
    me = lax.axis_index("dp")
    z = me // 2
    x = me % 2
    peer = 2 * z + 1 - x
    right = jnp.minimum(z + 1, line - 1) * 2 + x
    left = jnp.maximum(z - 1, 0) * 2 + x
    has_right = z < line - 1
    has_left = z > 0
    mirror = line - 1 - z

    def signal(sem, where):
        pl.semaphore_signal(
            sem, inc=1, device_id={"dp": where}, device_id_type=pl.DeviceIdType.MESH
        )

    barrier = pltpu.get_barrier_semaphore()
    mine = lax.axis_index("col")
    for offset in range(1, count):
        signal(barrier, lax.rem(me + offset, count))
    for offset in range(1, col_count):
        pl.semaphore_signal(
            barrier, inc=1, device_id={"col": lax.rem(mine + offset, col_count)},
            device_id_type=pl.DeviceIdType.MESH,
        )
    pl.semaphore_wait(barrier, count + col_count - 2)

    def remote(src, dst, send, recv, where):
        return pltpu.make_async_remote_copy(
            src_ref=src, dst_ref=dst, send_sem=send, recv_sem=recv,
            device_id={"dp": where}, device_id_type=pl.DeviceIdType.MESH,
        )

    def describe(item):
        layer = item // per_layer
        place = item % per_layer
        narrow = place % period == 0
        wide_at = place - (place + period - 1) // period
        narrow_at = place // period
        return layer, narrow, wide_at, narrow_at

    def x_copy(number):
        slot = number % XSLOTS
        return remote(xs.at[slot], xr.at[slot], xs_sem.at[slot], xr_sem.at[slot], peer)

    def r_copy(slot, target):
        return remote(
            part.at[slot, target], arr.at[slot, target + 1],
            rs_sem.at[slot, target], rr_sem.at[slot, target], right,
        )

    def l_copy(slot, target):
        return remote(
            part.at[slot, target], arr.at[slot, target],
            ls_sem.at[slot, target], ll_sem.at[slot, target], left,
        )

    def b_copy(number):
        return remote(
            bs.at[number], br.at[number], bs_sem.at[number], br_sem.at[number], peer
        )

    def product(layer, pair, target, start, width):
        return jnp.dot(
            cot_ref[layer, pair, target],
            act_ref[layer, :, pl.ds(pl.multiple_of(start, LANES), width)],
            preferred_element_type=jnp.float32,
        )

    def send_wide(item):
        layer, narrow, wide_at, _ = describe(item)

        @pl.when(jnp.logical_not(narrow))
        def _():
            number = layer * wide_per + wide_at
            slot = number % XSLOTS

            @pl.loop(0, line)
            def _(target):
                value = product(layer, 1 - x, target, wide_at * 2 * LANES, 2 * LANES)
                xs[slot, target, 0] = value[:, :LANES]
                xs[slot, target, 1] = value[:, LANES:]

            @pl.when(number >= XSLOTS)
            def _():
                pl.semaphore_wait(x_free, 1)

            x_copy(number).start()

    def form(item):
        layer, narrow, wide_at, narrow_at = describe(item)
        here = item % slots

        @pl.when(item >= slots)
        def _():
            @pl.when(has_right)
            def _():
                pl.semaphore_wait(from_right, 1)

            @pl.when(has_left)
            def _():
                pl.semaphore_wait(from_left, 1)

        @pl.when(narrow)
        def _():
            start = wide_per * 2 * LANES + narrow_at * LANES

            @pl.loop(0, line)
            def _(target):
                part[here, target, 0] = product(layer, 0, target, start, LANES)
                part[here, target, 1] = product(layer, 1, target, start, LANES)

        @pl.when(jnp.logical_not(narrow))
        def _():
            number = layer * wide_per + wide_at
            slot = number % XSLOTS
            x_copy(number).wait()

            @pl.loop(0, line)
            def _(target):
                value = product(layer, x, target, wide_at * 2 * LANES, 2 * LANES)
                part[here, target, 0] = value[:, :LANES] + xr[slot, target, 0]
                part[here, target, 1] = value[:, LANES:] + xr[slot, target, 1]

            @pl.when(number + XSLOTS < wides)
            def _():
                signal(x_free, peer)

    def hop(item, stage):
        here = item % slots

        @pl.when(z <= stage)
        def _():
            target = line - 1 - stage + z
            if stage > 0:
                @pl.when(has_left)
                def _():
                    r_copy(here, target).wait_recv()
                    part[here, target] += arr[here, target + 1]

            r_copy(here, target).start()

        @pl.when(mirror <= stage)
        def _():
            target = stage - mirror
            if stage > 0:
                @pl.when(has_right)
                def _():
                    l_copy(here, target).wait_recv()
                    part[here, target] += arr[here, target]

            l_copy(here, target).start()

    def finish(item):
        layer, narrow, wide_at, narrow_at = describe(item)
        here = item % slots

        @pl.when(has_left)
        def _():
            r_copy(here, z).wait_recv()
            part[here, z] += arr[here, z + 1]

        @pl.when(has_right)
        def _():
            l_copy(here, z).wait_recv()
            part[here, z] += arr[here, z]

        for target in range(line):
            @pl.when(target > z)
            def _(target=target):
                r_copy(here, target).wait_send()

            @pl.when(target < z)
            def _(target=target):
                l_copy(here, target).wait_send()

        @pl.when(narrow)
        def _():
            number = layer * 2 + narrow_at
            start = wide_per * 2 * LANES + narrow_at * LANES
            bs[number] = part[here, z, 1 - x]
            b_copy(number).start()
            out_ref[layer, :, pl.ds(pl.multiple_of(start, LANES), LANES)] = part[here, z, x]

        @pl.when(jnp.logical_not(narrow))
        def _():
            for half in range(2):
                start = wide_at * 2 * LANES + half * LANES
                out_ref[layer, :, pl.ds(pl.multiple_of(start, LANES), LANES)] = part[here, z, half]

        @pl.when(item + slots < items)
        def _():
            @pl.when(has_left)
            def _():
                signal(from_right, left)

            @pl.when(has_right)
            def _():
                signal(from_left, right)

    for item in range(1, AHEAD):
        send_wide(jnp.int32(item))

    @pl.loop(0, items + line - 1)
    def _(step):
        def guard(item, action):
            pl.when(jnp.logical_and(item >= 0, item < items))(lambda: action(item))

        guard(step + AHEAD, send_wide)
        guard(step - (line - 1), finish)
        for stage in reversed(range(1, line - 1)):
            guard(step - stage, functools.partial(hop, stage=stage))

        def begin(item):
            form(item)
            hop(item, 0)

        guard(step, begin)

    for number in range(2 * layers):
        b_copy(number).wait()
        start = wide_per * 2 * LANES + (number % 2) * LANES
        out_ref[number // 2, :, start : start + LANES] += br[number]

    def square_rows(index, total):
        layer = index // (rows // 8)
        at = pl.multiple_of(index % (rows // 8) * 8, 8)
        for piece in range(cols // LANES):
            value = out_ref[layer, pl.ds(at, 8), piece * LANES : (piece + 1) * LANES]
            total = total + value * value
        return total

    def spread(src, landing, send, recv, axis, index, size):
        copies = []
        for offset in range(1, size):
            copies.append(
                pltpu.make_async_remote_copy(
                    src_ref=src, dst_ref=landing.at[offset - 1],
                    send_sem=send.at[offset - 1], recv_sem=recv.at[offset - 1],
                    device_id={axis: lax.rem(index + offset, size)},
                    device_id_type=pl.DeviceIdType.MESH,
                )
            )
        for copy in copies:
            copy.start()
        for copy in copies:
            copy.wait()
        total = src[...]
        for offset in range(1, size):
            total = total + landing[offset - 1]
        return total

    own_sq[...] = lax.fori_loop(
        0, layers * rows // 8, square_rows, jnp.zeros((8, LANES), jnp.float32)
    )
    sum_sq[...] = spread(own_sq, col_sq, cs_sem, cr_sem, "col", mine, col_count)
    sq_ref[...] = spread(sum_sq, dp_sq, ds_sem, dr_sem, "dp", me, count)


def reduced_gradient(activations, cotangent, mesh_shape):
    count = mesh_shape["dp"]
    col_count = mesh_shape["col"]
    layers, tokens, cols = activations.shape
    line = count // 2
    rows = cotangent.shape[2] // count
    slots = line + 2
    cot = cotangent.reshape(layers, tokens, line, 2, rows).transpose(0, 3, 2, 4, 1)
    block = (line, 2, rows, LANES)
    dma = pltpu.SemaphoreType.DMA
    vmem = pl.BlockSpec(memory_space=pltpu.VMEM)
    return pl.pallas_call(
        functools.partial(reduce_kernel, count, col_count),
        out_shape=(
            jax.ShapeDtypeStruct((layers, rows, cols), jnp.float32),
            jax.ShapeDtypeStruct((8, LANES), jnp.float32),
        ),
        in_specs=[vmem, vmem],
        out_specs=(vmem, vmem),
        scratch_shapes=[
            pltpu.VMEM((XSLOTS,) + block, jnp.float32),
            pltpu.VMEM((XSLOTS,) + block, jnp.float32),
            pltpu.VMEM((slots,) + block, jnp.float32),
            pltpu.VMEM((slots, line + 1) + block[1:], jnp.float32),
            pltpu.VMEM((2 * layers, rows, LANES), jnp.float32),
            pltpu.VMEM((2 * layers, rows, LANES), jnp.float32),
            pltpu.VMEM((8, LANES), jnp.float32),
            pltpu.VMEM((8, LANES), jnp.float32),
            pltpu.VMEM((col_count - 1, 8, LANES), jnp.float32),
            pltpu.VMEM((count - 1, 8, LANES), jnp.float32),
            dma((XSLOTS,)), dma((XSLOTS,)),
            dma((slots, line)), dma((slots, line)), dma((slots, line)), dma((slots, line)),
            dma((2 * layers,)), dma((2 * layers,)),
            dma((col_count - 1,)), dma((col_count - 1,)), dma((count - 1,)), dma((count - 1,)),
            pltpu.SemaphoreType.REGULAR, pltpu.SemaphoreType.REGULAR, pltpu.SemaphoreType.REGULAR,
        ],
        compiler_params=pltpu.CompilerParams(
            collective_id=0, has_side_effects=True, vmem_limit_bytes=62 * 2**20
        ),
    )(cot, activations)


def local(
    mesh_shape, activations, cotangent, master_weights, moment_codes, square_codes, moment_scales, square_scales
):
    layer_count = activations.shape[0]
    shard_rows = master_weights.shape[1]
    shard_cols = master_weights.shape[2]
    block_count = moment_scales.shape[2]
    gradient, squares = reduced_gradient(activations, cotangent, mesh_shape)
    total_sq = jnp.sum(squares)
    rms = jnp.sqrt(total_sq / float(LAYERS * KV * D) + norm_eps)
    clip_factor = jnp.minimum(1.0, 1.0 / rms)
    correct_one = 1.0 - beta_one**STEP
    correct_two = 1.0 - beta_two**STEP
    own_block = lax.axis_index("col") * shard_cols // BLOCK
    selector = (jnp.arange(block_count, dtype=jnp.int32) == own_block).astype(jnp.float32)
    outs_weights, outs_mcode, outs_scode, outs_mscale, outs_sscale = ([], [], [], [], [])
    for layer_index in range(layer_count):
        moment_scale = jnp.sum(moment_scales[layer_index] * selector, axis=1)
        square_scale = jnp.sum(square_scales[layer_index] * selector, axis=1)
        old_moment = moment_codes[layer_index].astype(jnp.float32) * moment_scale[:, None]
        old_square = square_codes[layer_index].astype(jnp.float32) * square_scale[:, None]
        grad_now = clip_factor * gradient[layer_index]
        new_moment = beta_one * old_moment + (1.0 - beta_one) * grad_now
        new_square = beta_two * old_square + (1.0 - beta_two) * grad_now * grad_now
        moment_part = jnp.max(jnp.abs(new_moment), axis=1)[:, None] * selector
        square_part = jnp.max(new_square, axis=1)[:, None] * selector
        moment, square, moment_part, square_part = (
            new_moment,
            new_square,
            moment_part,
            square_part,
        )
        moment_max, square_max = lax.pmax((moment_part, square_part), "col")
        moment_div = jnp.sum(moment_max * selector, axis=1)[:, None]
        square_div = jnp.sum(square_max * selector, axis=1)[:, None]
        moment_out = (moment / (moment_div + scale_eps)).astype(jnp.bfloat16)
        square_out = (square / (square_div + scale_eps)).astype(jnp.bfloat16)
        ratio = moment / correct_one / (jnp.sqrt(square / correct_two) + adam_eps)
        weights = master_weights[layer_index]
        results = (weights - learn_rate * (decay_rate * weights + ratio), moment_out, square_out)
        outs_weights.append(results[0])
        outs_mcode.append(results[1])
        outs_scode.append(results[2])
        outs_mscale.append(moment_max)
        outs_sscale.append(square_max)
    return (
        jnp.stack(outs_weights),
        jnp.stack(outs_mcode),
        jnp.stack(outs_scode),
        jnp.stack(outs_mscale),
        jnp.stack(outs_sscale),
    )


def solution(mesh):
    in_specs = (
        P(None, "dp", "col"),
        P(None, "dp", None),
        P(None, "dp", "col"),
        P(None, "dp", "col"),
        P(None, "dp", "col"),
        P(None, "dp", None),
        P(None, "dp", None),
    )
    out_specs = (
        P(None, "dp", "col"),
        P(None, "dp", "col"),
        P(None, "dp", "col"),
        P(None, "dp", None),
        P(None, "dp", None),
    )
    return jax.shard_map(functools.partial(local, dict(mesh.shape)), mesh=mesh, in_specs=in_specs, out_specs=out_specs, check_vma=False)
```

profile of v0, /device:TPU:0, one launch (start us, length us, event | category | flops | bytes accessed | tf_op | source)
XLA Modules:
  0.0 429.3 jit_solution(12910254150144801660)
XLA Ops:
  0.7 0.8 fusion.28
  1.5 11.4 %copy.12 = bf16[2,896,2048]{1,2,0:T(8,128)(2,1)} copy(bf16[2,896,2048]{2,1,0:T(8,128)(2,1)} %param.8) | data formatting | bytes 14680064 | tf_op args[1]
  12.9 6.8 %copy.15 = bf16[2,896,4,2,256]{1,4,2,3,0:T(8,128)(2,1)} copy(bf16[2,896,4,2,256]{1,4,3,2,0:T(8,128)(2,1)} %bitcast.79) | data formatting | bytes 14680064 | tf_op jit(solution)/shard_map/reshape | solution.py:309
  19.7 375.7 %shard_map.110 = (f32[2,256,2048]{2,1,0:T(8,128)}, f32[8,128]{1,0:T(8,128)}) custom-call(bf16[2,2,4,256,896]{4,3,2,1,0:T(8,128)(2,1)} %bitcast.78, bf16[2,896,2048]{2,1,0:T(8,128)(2,1)} %act_ref.1), custom_call_target="tpu_custom_call" | custom-call | tf_op jit(solution)/shard_map/pallas_call | solution.py:313
  395.4 1.3 reduce_sum.82
  397.3 0.0 copy-start.1
  397.4 5.6 %fusion.12 = (f32[256]{0:T(256)S(1)}, f32[256]{0:T(256)S(1)}, f32[256]{0:T(256)S(1)}, f32[256]{0:T(256)S(1)}) fusion(f32[2,256,2048]{2,1,0:T(8,128)} %get-tuple-element.8, f32[256]{0:T(256)S(1)} %get-tuple-element.15, f32[]{:T(128)S(6)} %min.3, bf16[2,256,2048]{2,1,0:T(8,128)(2,1)} %param.11, f32[256]{0:T(256)S(1)} %get-tuple-element.16, ...), kind=kLoop, calls=%fused_computation.26 | loop fusion | flops 15727616 | bytes 8396804 | tf_op jit(solution)/shard_map/reduce_max | solution.py:369
  403.0 0.1 broadcast_multiply_fusion
  403.0 10.1 %all-reduce = (f32[256,4]{0,1:T(4,128)S(1)}, f32[256,4]{0,1:T(4,128)S(1)}, f32[256,4]{0,1:T(4,128)S(1)}, f32[256,4]{0,1:T(4,128)S(1)}) all-reduce(f32[256,4]{0,1:T(4,128)S(1)} %get-tuple-element.37, f32[256,4]{0,1:T(4,128)S(1)} %get-tuple-element.36, f32[256,4]{0,1:T(4,128)S(1)} %get-tuple-element.38, ...), channel_id=1, replica_groups=mesh['dp'=8,'col'=4] {'col'}, use_global_device_ids=true, to_apply=%region_12.13 | all-reduce | flops 4096 | bytes 32768 | tf_op jit(solution)/shard_map/pmax | solution.py:376
  413.2 0.1 multiply_reduce_fusion.1
  413.3 0.6 pad_maximum_fusion.3
  413.9 0.0 copy-done.1
  413.9 0.0 copy-start
  413.9 0.0 copy-start.2
  413.9 2.7 divide_convert_fusion.1
  416.6 0.4 copy-done
  417.0 0.7 copy-done.2
  417.7 6.3 %multiply_subtract_fusion.1 = (f32[1,256,2048]{2,1,0:T(8,128)S(1)}, f32[1,256,2048]{2,1,0:T(8,128)S(1)}, bf16[1,256,2048]{2,1,0:T(8,128)(2,1)S(1)}, bf16[1,256,2048]{2,1,0:T(8,128)(2,1)S(1)}) fusion(f32[2,256,2048]{2,1,0:T(8,128)} %param.9, f32[2,256,2048]{2,1,0:T(8,128)S(1)} %copy-done, f32[]{:T(128)S(6)} %min.3, f32[256]{0:T(256)S(1)} %get-tuple-element.24, ...), kind=kLoop, calls=%fused_computation.50 | loop fusion | flops 23068672 | bytes 18880516 | tf_op jit(solution)/shard_map/sub | solution.py:383
  424.0 2.3 pad_maximum_fusion
  426.3 1.5 pad_maximum_fusion.2
  427.8 1.5 pad_maximum_fusion.1
  (3 shorter events, 0.0 us)
Async XLA Ops:
  397.3 16.6 %copy-start.1 = (bf16[2,256,2048]{2,1,0:T(8,128)(2,1)S(1)}, bf16[2,256,2048]{2,1,0:T(8,128)(2,1)}, u32[]{:S(2)}) copy-start(bf16[2,256,2048]{2,1,0:T(8,128)(2,1)} %param.10) | copy-start | bytes 6291460
  413.9 3.1 copy-start
  413.9 3.8 copy-start.2
where the time goes:
time: 430 us; the launch traced here: 429 us
  Pallas kernels  376 us (87%)
  other arithmetic  22.7 us (5%)
  local copies, waits for them, and re-layouts  19.3 us (4%)
  blocking collectives  10.1 us (2%)
    pallas_call x1, Pallas kernels, reduced_gradient(): pl.pallas_call(functools.partial(reduce_kernel, count, col_count), out_sh...  376 us
    unnamed x7, local copies, waits for them, and re-layouts  12.5 us
    pmax x1, blocking collectives, local(): moment_max, square_max = lax.pmax((moment_part, square_part), 'col')  10.1 us

commit v1 on v0

--- a/solution.py
+++ b/solution.py
@@ -341,6 +341,522 @@
     )(cot, activations)
 
 
+AHEAD_UNITS = 5
+SEND_SLOTS = 6
+ACT_SLOTS = 5
+NARROW = 2
+
+
+def factor_kernel(
+    count, col_count, cot_hbm, act_hbm, out_ref, sq_ref,
+    cot_raw, act_raw, narrow_act, cot_t, act_cat, xs, xr, crx, part, arr, narrow_in,
+    own_sq, sum_sq, col_sq, dp_sq,
+    ld_sem, xs_sem, xr_sem, pr_sem, cs_sem, cr_sem, rs_sem, rr_sem, ls_sem, ll_sem, fs_sem, fr_sem,
+    qs_sem, qr_sem, ds_sem, dr_sem, act_free, cot_free, from_right, from_left,
+):
+    layers, tokens, cols = act_hbm.shape
+    half = cols // 2
+    line = count // 2
+    pair_rows = part.shape[2]
+    rows = pair_rows // 2
+    slots = part.shape[0]
+    chunks = half // LANES
+    first_chunks = chunks - NARROW // 2
+    wides = first_chunks + (layers - 1) * chunks
+    items = NARROW + wides
+    first_units = first_chunks + line
+    layer_units = chunks + line
+    units = first_units + (layers - 1) * layer_units
+    own = col_count - 1
+    me = lax.axis_index("dp")
+    mine = lax.axis_index("col")
+    z = me // 2
+    x = me % 2
+    peer = 2 * z + 1 - x
+    right = jnp.minimum(z + 1, line - 1) * 2 + x
+    left = jnp.maximum(z - 1, 0) * 2 + x
+    has_right = z < line - 1
+    has_left = z > 0
+    mirror = line - 1 - z
+    own_half = pl.multiple_of(x * half, LANES)
+    peer_half = pl.multiple_of((1 - x) * half, LANES)
+
+    def lanes(start, width=LANES):
+        return pl.ds(pl.multiple_of(start, LANES), width)
+
+    def signal(sem, where):
+        pl.semaphore_signal(
+            sem, inc=1, device_id={"dp": where}, device_id_type=pl.DeviceIdType.MESH
+        )
+
+    loads = []
+
+    def load(src, dst):
+        copy = pltpu.make_async_copy(src, dst, ld_sem.at[len(loads)])
+        copy.start()
+        loads.append(copy)
+
+    load(cot_hbm.at[0], cot_raw.at[0])
+    for index in range(NARROW):
+        start = (index % 2) * half + (chunks - 1 - index // 2) * LANES
+        load(act_hbm.at[0, :, lanes(start)], narrow_act.at[index])
+    for layer in range(layers):
+        if layer > 0:
+            load(cot_hbm.at[layer], cot_raw.at[layer])
+        load(act_hbm.at[layer, :, pl.ds(peer_half, half)], act_raw.at[layer])
+        load(act_hbm.at[layer, :, pl.ds(own_half, half)], act_cat.at[layer, pl.ds(0, tokens)])
+
+    barrier = pltpu.get_barrier_semaphore()
+    for offset in range(1, count):
+        signal(barrier, lax.rem(me + offset, count))
+    for offset in range(1, col_count):
+        pl.semaphore_signal(
+            barrier, inc=1, device_id={"col": lax.rem(mine + offset, col_count)},
+            device_id_type=pl.DeviceIdType.MESH,
+        )
+    pl.semaphore_wait(barrier, count + col_count - 2)
+
+    def remote(src, dst, send, recv, where):
+        return pltpu.make_async_remote_copy(
+            src_ref=src, dst_ref=dst, send_sem=send, recv_sem=recv,
+            device_id={"dp": where}, device_id_type=pl.DeviceIdType.MESH,
+        )
+
+    def block_target(place):
+        after = line - 1 - z
+        rising = jnp.where(place < after, line - 1 - place, place - after)
+        falling = jnp.where(place < z, place, line - 1 - (place - z))
+        other = jnp.where(z < line // 2, rising, falling)
+        return jnp.where(place < line - 1, other, z)
+
+    def describe(item):
+        number = item - NARROW
+        narrow = item < NARROW
+        later = jnp.maximum(number - first_chunks, 0)
+        layer = jnp.where(number < first_chunks, 0, 1 + later // chunks)
+        chunk = jnp.where(number < first_chunks, number, later % chunks)
+        return layer, narrow, chunk
+
+    def unit_base(layer):
+        return jnp.where(layer == 0, 0, first_units + (layer - 1) * layer_units)
+
+    def act_number(layer, chunk):
+        return jnp.where(layer == 0, chunk, first_chunks + (layer - 1) * chunks + chunk)
+
+    def act_copy(unit, number):
+        here = unit % SEND_SLOTS
+        slot = number % ACT_SLOTS
+        return remote(xs.at[here], xr.at[slot], xs_sem.at[here], xr_sem.at[slot], peer)
+
+    def cot_copy(unit, place):
+        here = unit % SEND_SLOTS
+        return remote(xs.at[here], crx.at[place, own], xs_sem.at[here], pr_sem.at[place], peer)
+
+    def col_copy(place, offset):
+        return pltpu.make_async_remote_copy(
+            src_ref=crx.at[place, own], dst_ref=crx.at[place, offset - 1],
+            send_sem=cs_sem.at[place, offset - 1], recv_sem=cr_sem.at[place, offset - 1],
+            device_id={"col": lax.rem(mine + offset, col_count)},
+            device_id_type=pl.DeviceIdType.MESH,
+        )
+
+    def r_copy(slot, target):
+        return remote(
+            part.at[slot, target], arr.at[slot, target + 1],
+            rs_sem.at[slot, target], rr_sem.at[slot, target], right,
+        )
+
+    def l_copy(slot, target):
+        return remote(
+            part.at[slot, target], arr.at[slot, target],
+            ls_sem.at[slot, target], ll_sem.at[slot, target], left,
+        )
+
+    def row_source(slot):
+        return part.at[slot, z, pl.ds(pl.multiple_of((1 - x) * rows, 8), rows)]
+
+    def n_copy(item):
+        slot = item % slots
+        return remote(
+            row_source(slot), narrow_in.at[jnp.minimum(item, NARROW - 1)],
+            fs_sem.at[slot], fr_sem.at[item], peer,
+        )
+
+    def f_copy(item, side):
+        layer, narrow, chunk = describe(item)
+        slot = item % slots
+        where = out_ref.at[layer, :, lanes(side * half + chunk * LANES)]
+        return remote(row_source(slot), where, fs_sem.at[slot], fr_sem.at[item], peer)
+
+    def send(unit):
+        @pl.when(unit < units)
+        def _():
+            layer = jnp.where(unit < first_units, 0, 1 + (unit - first_units) // layer_units)
+            index = unit - unit_base(layer)
+            is_cot = jnp.logical_or(index < line - 1, index == 2 * line - 2)
+            here = unit % SEND_SLOTS
+
+            @pl.when(unit >= SEND_SLOTS)
+            def _():
+                act_copy(unit, 0).wait_send()
+
+            @pl.when(is_cot)
+            def _():
+                place = jnp.minimum(index, line - 1)
+                start = block_target(place) * pair_rows + mine * LANES
+                xs[here] = cot_raw[layer, :, lanes(start)].astype(jnp.float32)
+
+                @pl.when(layer > 0)
+                def _():
+                    pl.semaphore_wait(cot_free.at[place], 1)
+
+                cot_copy(unit, place).start()
+
+            @pl.when(jnp.logical_not(is_cot))
+            def _():
+                chunk = jnp.where(index < 2 * line - 2, index - (line - 1), index - line)
+                number = act_number(layer, chunk)
+                xs[here] = act_raw[layer, :, lanes(chunk * LANES)].astype(jnp.float32)
+
+                @pl.when(number >= ACT_SLOTS)
+                def _():
+                    pl.semaphore_wait(act_free.at[number % ACT_SLOTS], 1)
+
+                act_copy(unit, number).start()
+
+    def forward(layer, place):
+        cot_copy(0, place).wait_recv()
+        for offset in range(1, col_count):
+            col_copy(place, offset).start()
+        send(unit_base(layer) + jnp.where(place < line - 1, place, 2 * line - 2) + AHEAD_UNITS)
+
+    def prepare(layer, place):
+        base = block_target(place) * pair_rows
+
+        @pl.loop(0, col_count)
+        def _(member):
+            start = base + member * LANES
+            value = cot_raw[layer, :, lanes(start)].astype(jnp.float32)
+            cot_t[layer, lanes(start), pl.ds(0, tokens)] = value.T.astype(jnp.bfloat16)
+
+    def absorb(layer, place):
+        @pl.when(layer > 0)
+        def _():
+            prepare(layer, place)
+
+        base = block_target(place) * pair_rows
+        for offset in range(col_count):
+            if offset > 0:
+                col_copy(place, offset).wait_recv()
+            source = crx[place, offset - 1 if offset > 0 else own]
+            owner = lax.rem(mine - offset + col_count, col_count)
+            cot_t[layer, lanes(base + owner * LANES), pl.ds(tokens, tokens)] = source.T.astype(jnp.bfloat16)
+        for offset in range(1, col_count):
+            col_copy(place, offset).wait_send()
+
+        @pl.when(layer < layers - 1)
+        def _():
+            signal(cot_free.at[place], peer)
+
+    def take(layer, chunk):
+        number = act_number(layer, chunk)
+        slot = number % ACT_SLOTS
+        act_copy(0, number).wait_recv()
+        act_cat[layer, pl.ds(tokens, tokens), lanes(chunk * LANES)] = xr[slot].astype(jnp.bfloat16)
+
+        @pl.when(number + ACT_SLOTS < wides)
+        def _():
+            signal(act_free.at[slot], peer)
+
+        index = jnp.where(chunk < line - 1, chunk + line - 1, chunk + line)
+        send(unit_base(layer) + index + AHEAD_UNITS)
+
+    def form(item, target):
+        layer, narrow, chunk = describe(item)
+        here = item % slots
+        at = pl.ds(pl.multiple_of(target * pair_rows, LANES), pair_rows)
+
+        @pl.when(narrow)
+        def _():
+            part[here, target] = jnp.dot(
+                cot_t[0, at, pl.ds(0, tokens)], narrow_act[jnp.minimum(item, NARROW - 1)],
+                preferred_element_type=jnp.float32,
+            )
+
+        @pl.when(jnp.logical_not(narrow))
+        def _():
+            part[here, target] = jnp.dot(
+                cot_t[layer, at, :], act_cat[layer, :, lanes(chunk * LANES)],
+                preferred_element_type=jnp.float32,
+            )
+
+    def opens(item):
+        layer, narrow, chunk = describe(item)
+        return layer, jnp.logical_and(jnp.logical_not(narrow), chunk == 0)
+
+    def ready(item, place):
+        @pl.when(item == 0)
+        def _():
+            prepare(0, place)
+
+        layer, first = opens(item)
+
+        @pl.when(first)
+        def _():
+            if place == 0:
+                for early in range(2, line - 1):
+                    forward(layer, early)
+            absorb(layer, place)
+
+    def hop(item, stage):
+        here = item % slots
+
+        @pl.when(z <= stage)
+        def _():
+            target = line - 1 - stage + z
+            form(item, target)
+            if stage > 0:
+                @pl.when(has_left)
+                def _():
+                    r_copy(here, target).wait_recv()
+                    part[here, target] += arr[here, target + 1]
+
+            r_copy(here, target).start()
+
+        @pl.when(mirror <= stage)
+        def _():
+            target = stage - mirror
+            form(item, target)
+            if stage > 0:
+                @pl.when(has_right)
+                def _():
+                    l_copy(here, target).wait_recv()
+                    part[here, target] += arr[here, target]
+
+            l_copy(here, target).start()
+
+    def begin(item):
+        layer, narrow, chunk = describe(item)
+        ready(item, 0)
+
+        @pl.when(jnp.logical_not(narrow))
+        def _():
+            take(layer, chunk)
+
+        @pl.when(item >= slots)
+        def _():
+            @pl.when(has_right)
+            def _():
+                pl.semaphore_wait(from_right, 1)
+
+            @pl.when(has_left)
+            def _():
+                pl.semaphore_wait(from_left, 1)
+
+        hop(item, 0)
+        next_layer, next_first = opens(item + 1)
+
+        @pl.when(jnp.logical_and(next_first, item + 1 < items))
+        def _():
+            for place in range(2):
+                forward(next_layer, place)
+
+        @pl.when(jnp.logical_and(jnp.logical_not(narrow), chunk == line - 2))
+        def _():
+            forward(layer, line - 1)
+
+    def middle(item, stage):
+        ready(item, stage)
+        hop(item, stage)
+
+    def finish(item):
+        layer, narrow, chunk = describe(item)
+        here = item % slots
+        ready(item, line - 1)
+
+        @pl.when(item >= slots)
+        def _():
+            n_copy(item - slots).wait_send()
+
+        form(item, z)
+
+        @pl.when(has_left)
+        def _():
+            r_copy(here, z).wait_recv()
+            part[here, z] += arr[here, z + 1]
+
+        @pl.when(has_right)
+        def _():
+            l_copy(here, z).wait_recv()
+            part[here, z] += arr[here, z]
+
+        for target in range(line):
+            @pl.when(target > z)
+            def _(target=target):
+                r_copy(here, target).wait_send()
+
+            @pl.when(target < z)
+            def _(target=target):
+                l_copy(here, target).wait_send()
+
+        kept = pl.ds(pl.multiple_of(x * rows, 8), rows)
+
+        @pl.when(narrow)
+        def _():
+            n_copy(item).start()
+            start = (item % 2) * half + (chunks - 1 - item // 2) * LANES
+            out_ref[0, :, lanes(start)] = part[here, z, kept]
+
+        @pl.when(jnp.logical_not(narrow))
+        def _():
+            f_copy(item, x).start()
+            out_ref[layer, :, lanes(own_half + chunk * LANES)] = part[here, z, kept]
+
+        @pl.when(item + slots < items)
+        def _():
+            @pl.when(has_left)
+            def _():
+                signal(from_right, left)
+
+            @pl.when(has_right)
+            def _():
+                signal(from_left, right)
+
+    for copy in loads[: 2 + NARROW]:
+        copy.wait()
+
+    @pl.loop(0, AHEAD_UNITS)
+    def _(unit):
+        send(unit)
+
+    for copy in loads[2 + NARROW :]:
+        copy.wait()
+
+    @pl.loop(0, items + line - 1)
+    def _(step):
+        def guard(item, action):
+            pl.when(jnp.logical_and(item >= 0, item < items))(lambda: action(item))
+
+        for stage in reversed(range(1, line - 1)):
+            guard(step - stage, functools.partial(middle, stage=stage))
+        guard(step, begin)
+        guard(step - (line - 1), finish)
+
+    @pl.loop(units - SEND_SLOTS, units)
+    def _(unit):
+        act_copy(unit, 0).wait_send()
+
+    @pl.loop(items - slots, items)
+    def _(item):
+        n_copy(item).wait_send()
+
+    for item in range(NARROW):
+        n_copy(item).wait_recv()
+        start = (item % 2) * half + (chunks - 1 - item // 2) * LANES
+        out_ref[0, :, start : start + LANES] += narrow_in[item]
+
+    @pl.loop(NARROW, items)
+    def _(item):
+        f_copy(item, 1 - x).wait_recv()
+
+    def square_rows(index, total):
+        layer = index // (rows // 8)
+        at = pl.multiple_of(index % (rows // 8) * 8, 8)
+        for piece in range(cols // LANES):
+            value = out_ref[layer, pl.ds(at, 8), piece * LANES : (piece + 1) * LANES]
+            total = total + value * value
+        return total
+
+    def spread(src, landing, send_sems, recv_sems, axis, index, size):
+        copies = []
+        for offset in range(1, size):
+            copies.append(
+                pltpu.make_async_remote_copy(
+                    src_ref=src, dst_ref=landing.at[offset - 1],
+                    send_sem=send_sems.at[offset - 1], recv_sem=recv_sems.at[offset - 1],
+                    device_id={axis: lax.rem(index + offset, size)},
+                    device_id_type=pl.DeviceIdType.MESH,
+                )
+            )
+        for copy in copies:
+            copy.start()
+        for copy in copies:
+            copy.wait()
+        total = src[...]
+        for offset in range(1, size):
+            total = total + landing[offset - 1]
+        return total
+
+    own_sq[...] = lax.fori_loop(
+        0, layers * rows // 8, square_rows, jnp.zeros((8, LANES), jnp.float32)
+    )
+    sum_sq[...] = spread(own_sq, col_sq, qs_sem, qr_sem, "col", mine, col_count)
+    sq_ref[...] = spread(sum_sq, dp_sq, ds_sem, dr_sem, "dp", me, count)
+
+
+def factor_gradient(activations, cotangent, mesh_shape):
+    count = mesh_shape["dp"]
+    col_count = mesh_shape["col"]
+    layers, tokens, cols = activations.shape
+    line = count // 2
+    features = cotangent.shape[2]
+    rows = features // count
+    half = cols // 2
+    slots = line + 1
+    items = NARROW + layers * (half // LANES) - NARROW // 2
+    piece = (tokens, LANES)
+    f32, bf16 = jnp.float32, jnp.bfloat16
+    dma = pltpu.SemaphoreType.DMA
+    regular = pltpu.SemaphoreType.REGULAR
+    vmem = pl.BlockSpec(memory_space=pltpu.VMEM)
+    hbm = pl.BlockSpec(memory_space=pl.ANY)
+    return pl.pallas_call(
+        functools.partial(factor_kernel, count, col_count),
+        out_shape=(
+            jax.ShapeDtypeStruct((layers, rows, cols), f32),
+            jax.ShapeDtypeStruct((8, LANES), f32),
+        ),
+        in_specs=[hbm, hbm],
+        out_specs=(vmem, vmem),
+        scratch_shapes=[
+            pltpu.VMEM((layers, tokens, features), bf16),
+            pltpu.VMEM((layers, tokens, half), bf16),
+            pltpu.VMEM((NARROW,) + piece, bf16),
+            pltpu.VMEM((layers, features, 2 * tokens), bf16),
+            pltpu.VMEM((layers, 2 * tokens, half), bf16),
+            pltpu.VMEM((SEND_SLOTS,) + piece, f32),
+            pltpu.VMEM((ACT_SLOTS,) + piece, f32),
+            pltpu.VMEM((line, col_count) + piece, f32),
+            pltpu.VMEM((slots, line, 2 * rows, LANES), f32),
+            pltpu.VMEM((slots, line + 1, 2 * rows, LANES), f32),
+            pltpu.VMEM((NARROW, rows, LANES), f32),
+            pltpu.VMEM((8, LANES), f32),
+            pltpu.VMEM((8, LANES), f32),
+            pltpu.VMEM((col_count - 1, 8, LANES), f32),
+            pltpu.VMEM((count - 1, 8, LANES), f32),
+            dma((NARROW + 3 * layers,)),
+            dma((SEND_SLOTS,)), dma((ACT_SLOTS,)), dma((line,)),
+            dma((line, col_count - 1)), dma((line, col_count - 1)),
+            dma((slots, line)), dma((slots, line)), dma((slots, line)), dma((slots, line)),
+            dma((slots,)), dma((items,)),
+            dma((col_count - 1,)), dma((col_count - 1,)), dma((count - 1,)), dma((count - 1,)),
+            regular((ACT_SLOTS,)), regular((line,)), regular, regular,
+        ],
+        compiler_params=pltpu.CompilerParams(
+            collective_id=0, has_side_effects=True, vmem_limit_bytes=62 * 2**20
+        ),
+    )(cotangent, activations)
+
+
+def fits_factors(activations, cotangent, mesh_shape):
+    count = mesh_shape["dp"]
+    line = count // 2
+    rows = cotangent.shape[2] // count
+    chunks = activations.shape[2] // (2 * LANES)
+    aligned = activations.shape[1] % LANES == 0 and activations.shape[2] % (2 * LANES) == 0
+    return aligned and line >= 3 and 2 * rows == LANES * mesh_shape["col"] and chunks - NARROW // 2 > line
+
+
 def local(
     mesh_shape, activations, cotangent, master_weights, moment_codes, square_codes, moment_scales, square_scales
 ):
@@ -348,7 +864,8 @@
     shard_rows = master_weights.shape[1]
     shard_cols = master_weights.shape[2]
     block_count = moment_scales.shape[2]
-    gradient, squares = reduced_gradient(activations, cotangent, mesh_shape)
+    reduce = factor_gradient if fits_factors(activations, cotangent, mesh_shape) else reduced_gradient
+    gradient, squares = reduce(activations, cotangent, mesh_shape)
     total_sq = jnp.sum(squares)
     rms = jnp.sqrt(total_sq / float(LAYERS * KV * D) + norm_eps)
     clip_factor = jnp.minimum(1.0, 1.0 / rms)

time: 430 us -> 369 us (0.86)
  Pallas kernels: 376 us -> 334 us
  local copies, waits for them, and re-layouts: 19.3 us -> 1.11 us
    pallas_call x1, Pallas kernels: 376 us -> 334 us  [factor_gradient(): pl.pallas_call(functools.partial(factor_kernel, count, col_count), out_sh...]
    unnamed x7 -> x6, local copies, waits for them, and re-layouts: 12.5 us -> 1.11 us
    reshape x1 -> x0, local copies, waits for them, and re-layouts: 6.84 us -> none  [reduced_gradient(): cotangent.reshape(layers, tokens, line, 2, rows).transpose(0, 3, 2, 4, 1)]
where the time goes in v1:
time: 369 us
  Pallas kernels  334 us (91%)
  other arithmetic  22.8 us (6%)
  blocking collectives  10.1 us (3%)
    pallas_call x1, Pallas kernels, factor_gradient(): pl.pallas_call(functools.partial(factor_kernel, count, col_count), out_sh...  334 us
    pmax x1, blocking collectives, local(): moment_max, square_max = lax.pmax((moment_part, square_part), 'col')  10.1 us

profile of v1, /device:TPU:0, one launch (start us, length us, event | category | flops | bytes accessed | tf_op | source)
XLA Modules:
  0.0 369.0 jit_solution(7960854642163980747)
XLA Ops:
  0.7 0.8 fusion.28
  1.5 333.5 %shard_map.110 = (f32[2,256,2048]{2,1,0:T(8,128)}, f32[8,128]{1,0:T(8,128)}) custom-call(bf16[2,896,2048]{2,1,0:T(8,128)(2,1)} %cot_hbm.1, bf16[2,896,2048]{2,1,0:T(8,128)(2,1)} %act_hbm.1), custom_call_target="tpu_custom_call" | custom-call | tf_op jit(solution)/shard_map/pallas_call | solution.py:813
  335.0 1.3 reduce_sum.82
  337.0 0.0 copy-start.1
  337.0 5.7 %fusion.12 = (f32[256]{0:T(256)S(1)}, f32[256]{0:T(256)S(1)}, f32[256]{0:T(256)S(1)}, f32[256]{0:T(256)S(1)}) fusion(f32[2,256,2048]{2,1,0:T(8,128)} %get-tuple-element.8, f32[256]{0:T(256)S(1)} %get-tuple-element.15, f32[]{:T(128)S(6)} %min.3, bf16[2,256,2048]{2,1,0:T(8,128)(2,1)} %param.11, f32[256]{0:T(256)S(1)} %get-tuple-element.16, ...), kind=kLoop, calls=%fused_computation.25 | loop fusion | flops 15727616 | bytes 8396804 | tf_op jit(solution)/shard_map/reduce_max | solution.py:886
  342.7 0.1 broadcast_multiply_fusion
  342.8 10.1 %all-reduce = (f32[256,4]{0,1:T(4,128)S(1)}, f32[256,4]{0,1:T(4,128)S(1)}, f32[256,4]{0,1:T(4,128)S(1)}, f32[256,4]{0,1:T(4,128)S(1)}) all-reduce(f32[256,4]{0,1:T(4,128)S(1)} %get-tuple-element.37, f32[256,4]{0,1:T(4,128)S(1)} %get-tuple-element.36, f32[256,4]{0,1:T(4,128)S(1)} %get-tuple-element.38, ...), channel_id=1, replica_groups=mesh['dp'=8,'col'=4] {'col'}, use_global_device_ids=true, to_apply=%region_12.13 | all-reduce | flops 4096 | bytes 32768 | tf_op jit(solution)/shard_map/pmax | solution.py:893
  352.9 0.1 multiply_reduce_fusion.1
  353.0 0.6 pad_maximum_fusion.3
  353.6 0.0 copy-done.1
  353.6 0.0 copy-start
  353.6 0.0 copy-start.2
  353.6 2.7 divide_convert_fusion.1
  356.4 0.4 copy-done
  356.8 0.7 copy-done.2
  357.5 6.3 %multiply_subtract_fusion.1 = (f32[1,256,2048]{2,1,0:T(8,128)S(1)}, f32[1,256,2048]{2,1,0:T(8,128)S(1)}, bf16[1,256,2048]{2,1,0:T(8,128)(2,1)S(1)}, bf16[1,256,2048]{2,1,0:T(8,128)(2,1)S(1)}) fusion(f32[2,256,2048]{2,1,0:T(8,128)} %param.9, f32[2,256,2048]{2,1,0:T(8,128)S(1)} %copy-done, f32[]{:T(128)S(6)} %min.3, f32[256]{0:T(256)S(1)} %get-tuple-element.24, ...), kind=kLoop, calls=%fused_computation.49 | loop fusion | flops 23068672 | bytes 18880516 | tf_op jit(solution)/shard_map/sub | solution.py:900
  363.7 2.3 pad_maximum_fusion
  366.0 1.5 pad_maximum_fusion.2
  367.5 1.5 pad_maximum_fusion.1
  (3 shorter events, 0.0 us)
Async XLA Ops:
  337.0 16.6 %copy-start.1 = (bf16[2,256,2048]{2,1,0:T(8,128)(2,1)S(1)}, bf16[2,256,2048]{2,1,0:T(8,128)(2,1)}, u32[]{:S(2)}) copy-start(bf16[2,256,2048]{2,1,0:T(8,128)(2,1)} %param.10) | copy-start | bytes 6291460
  353.6 3.1 copy-start
  353.6 3.8 %copy-start.2 = (bf16[2,256,2048]{2,1,0:T(8,128)(2,1)S(1)}, bf16[2,256,2048]{2,1,0:T(8,128)(2,1)}, u32[]{:S(2)}) copy-start(bf16[2,256,2048]{2,1,0:T(8,128)(2,1)} %param.11) | copy-start | bytes 6291460

commit v2 on v1

--- a/solution.py
+++ b/solution.py
@@ -345,11 +345,12 @@
 SEND_SLOTS = 6
 ACT_SLOTS = 5
 NARROW = 2
+RELEASE = 3
 
 
 def factor_kernel(
     count, col_count, cot_hbm, act_hbm, out_ref, sq_ref,
-    cot_raw, act_raw, narrow_act, cot_t, act_cat, xs, xr, crx, part, arr, narrow_in,
+    cot_raw, act_raw, narrow_act, cot_t, act_cat, xs, xr, crx, part, arr, narrow_in, held,
     own_sq, sum_sq, col_sq, dp_sq,
     ld_sem, xs_sem, xr_sem, pr_sem, cs_sem, cr_sem, rs_sem, rr_sem, ls_sem, ll_sem, fs_sem, fr_sem,
     qs_sem, qr_sem, ds_sem, dr_sem, act_free, cot_free, from_right, from_left,
@@ -367,12 +368,14 @@
     first_units = first_chunks + line
     layer_units = chunks + line
     units = first_units + (layers - 1) * layer_units
-    own = col_count - 1
+    all_sent = items - chunks + line - 2
+    groups = col_count // 2
     me = lax.axis_index("dp")
     mine = lax.axis_index("col")
     z = me // 2
     x = me % 2
     peer = 2 * z + 1 - x
+    partner = mine + 1 - 2 * (mine % 2)
     right = jnp.minimum(z + 1, line - 1) * 2 + x
     left = jnp.maximum(z - 1, 0) * 2 + x
     has_right = z < line - 1
@@ -396,15 +399,27 @@
         copy.start()
         loads.append(copy)
 
-    load(cot_hbm.at[0], cot_raw.at[0])
+    def block_target(place):
+        after = line - 1 - z
+        rising = jnp.where(place < after, line - 1 - place, place - after)
+        falling = jnp.where(place < z, place, line - 1 - (place - z))
+        other = jnp.where(z < line // 2, rising, falling)
+        return jnp.where(place < line - 1, other, z)
+
+    for place in range(line):
+        block = lanes(block_target(place) * pair_rows, pair_rows)
+        load(cot_hbm.at[0, :, block], cot_raw.at[0, :, block])
+    load(act_hbm.at[0, :, pl.ds(peer_half, half)], act_raw.at[0])
     for index in range(NARROW):
         start = (index % 2) * half + (chunks - 1 - index // 2) * LANES
         load(act_hbm.at[0, :, lanes(start)], narrow_act.at[index])
     for layer in range(layers):
         if layer > 0:
             load(cot_hbm.at[layer], cot_raw.at[layer])
-        load(act_hbm.at[layer, :, pl.ds(peer_half, half)], act_raw.at[layer])
+            load(act_hbm.at[layer, :, pl.ds(peer_half, half)], act_raw.at[layer])
         load(act_hbm.at[layer, :, pl.ds(own_half, half)], act_cat.at[layer, pl.ds(0, tokens)])
+
+    early_loads = line + 1 + NARROW
 
     barrier = pltpu.get_barrier_semaphore()
     for offset in range(1, count):
@@ -422,13 +437,6 @@
             device_id={"dp": where}, device_id_type=pl.DeviceIdType.MESH,
         )
 
-    def block_target(place):
-        after = line - 1 - z
-        rising = jnp.where(place < after, line - 1 - place, place - after)
-        falling = jnp.where(place < z, place, line - 1 - (place - z))
-        other = jnp.where(z < line // 2, rising, falling)
-        return jnp.where(place < line - 1, other, z)
-
     def describe(item):
         number = item - NARROW
         narrow = item < NARROW
@@ -450,15 +458,17 @@
 
     def cot_copy(unit, place):
         here = unit % SEND_SLOTS
-        return remote(xs.at[here], crx.at[place, own], xs_sem.at[here], pr_sem.at[place], peer)
-
-    def col_copy(place, offset):
+        return remote(xs.at[here], crx.at[place, mine], xs_sem.at[here], pr_sem.at[place], peer)
+
+    def col_copy(place, owner, number, where):
         return pltpu.make_async_remote_copy(
-            src_ref=crx.at[place, own], dst_ref=crx.at[place, offset - 1],
-            send_sem=cs_sem.at[place, offset - 1], recv_sem=cr_sem.at[place, offset - 1],
-            device_id={"col": lax.rem(mine + offset, col_count)},
-            device_id_type=pl.DeviceIdType.MESH,
-        )
+            src_ref=crx.at[place, owner], dst_ref=crx.at[place, owner],
+            send_sem=cs_sem.at[place, number], recv_sem=cr_sem.at[place, owner],
+            device_id={"col": where}, device_id_type=pl.DeviceIdType.MESH,
+        )
+
+    def far(index):
+        return lax.rem(mine + 2 * index, col_count)
 
     def r_copy(slot, target):
         return remote(
@@ -472,21 +482,27 @@
             ls_sem.at[slot, target], ll_sem.at[slot, target], left,
         )
 
-    def row_source(slot):
-        return part.at[slot, z, pl.ds(pl.multiple_of((1 - x) * rows, 8), rows)]
-
     def n_copy(item):
-        slot = item % slots
-        return remote(
-            row_source(slot), narrow_in.at[jnp.minimum(item, NARROW - 1)],
-            fs_sem.at[slot], fr_sem.at[item], peer,
-        )
+        where = narrow_in.at[jnp.minimum(item, NARROW - 1)]
+        return remote(held.at[item], where, fs_sem.at[item], fr_sem.at[item], peer)
 
     def f_copy(item, side):
         layer, narrow, chunk = describe(item)
-        slot = item % slots
         where = out_ref.at[layer, :, lanes(side * half + chunk * LANES)]
-        return remote(row_source(slot), where, fs_sem.at[slot], fr_sem.at[item], peer)
+        return remote(held.at[item], where, fs_sem.at[item], fr_sem.at[item], peer)
+
+    def exchange(item):
+        @pl.when(item < NARROW)
+        def _():
+            n_copy(item).start()
+
+        @pl.when(item >= NARROW)
+        def _():
+            f_copy(item, x).start()
+
+    def exchanged(step):
+        done = jnp.minimum(step - (line - 1), RELEASE * (step - 1 - all_sent))
+        return jnp.clip(done, 0, items)
 
     def send(unit):
         @pl.when(unit < units)
@@ -526,9 +542,15 @@
 
     def forward(layer, place):
         cot_copy(0, place).wait_recv()
-        for offset in range(1, col_count):
-            col_copy(place, offset).start()
+        for index in range(1, groups):
+            col_copy(place, mine, index, far(index)).start()
+        col_copy(place, mine, 0, partner).start()
         send(unit_base(layer) + jnp.where(place < line - 1, place, 2 * line - 2) + AHEAD_UNITS)
+
+    def relay(place):
+        for index in range(1, groups):
+            col_copy(place, far(index), groups - 1 + index, partner).wait_recv()
+            col_copy(place, far(index), groups - 1 + index, partner).start()
 
     def prepare(layer, place):
         base = block_target(place) * pair_rows
@@ -545,14 +567,17 @@
             prepare(layer, place)
 
         base = block_target(place) * pair_rows
-        for offset in range(col_count):
-            if offset > 0:
-                col_copy(place, offset).wait_recv()
-            source = crx[place, offset - 1 if offset > 0 else own]
-            owner = lax.rem(mine - offset + col_count, col_count)
+        col_copy(place, partner, 0, partner).wait_recv()
+        for index in range(1, groups):
+            col_copy(place, lax.rem(partner + 2 * index, col_count), 0, partner).wait_recv()
+
+        @pl.loop(0, col_count)
+        def _(owner):
+            source = crx[place, owner]
             cot_t[layer, lanes(base + owner * LANES), pl.ds(tokens, tokens)] = source.T.astype(jnp.bfloat16)
-        for offset in range(1, col_count):
-            col_copy(place, offset).wait_send()
+
+        for number in range(col_count - 1):
+            col_copy(place, mine, number, partner).wait_send()
 
         @pl.when(layer < layers - 1)
         def _():
@@ -604,8 +629,17 @@
         @pl.when(first)
         def _():
             if place == 0:
+                @pl.when(layer == 0)
+                def _():
+                    for early in range(2):
+                        forward(layer, early)
+
                 for early in range(2, line - 1):
                     forward(layer, early)
+                for early in range(2):
+                    relay(early)
+            if place == line - 1:
+                relay(place)
             absorb(layer, place)
 
     def hop(item, stage):
@@ -654,9 +688,20 @@
                 pl.semaphore_wait(from_left, 1)
 
         hop(item, 0)
+
+        @pl.when(item == 1)
+        def _():
+            for copy in loads[early_loads:]:
+                copy.wait()
+
+        @pl.when(jnp.logical_and(jnp.logical_not(narrow), chunk == 0))
+        def _():
+            for early in range(2, line - 1):
+                relay(early)
+
         next_layer, next_first = opens(item + 1)
 
-        @pl.when(jnp.logical_and(next_first, item + 1 < items))
+        @pl.when(jnp.logical_and(next_first, jnp.logical_and(next_layer > 0, item + 1 < items)))
         def _():
             for place in range(2):
                 forward(next_layer, place)
@@ -674,10 +719,6 @@
         here = item % slots
         ready(item, line - 1)
 
-        @pl.when(item >= slots)
-        def _():
-            n_copy(item - slots).wait_send()
-
         form(item, z)
 
         @pl.when(has_left)
@@ -700,16 +741,15 @@
                 l_copy(here, target).wait_send()
 
         kept = pl.ds(pl.multiple_of(x * rows, 8), rows)
+        held[item] = part[here, z, pl.ds(pl.multiple_of((1 - x) * rows, 8), rows)]
 
         @pl.when(narrow)
         def _():
-            n_copy(item).start()
             start = (item % 2) * half + (chunks - 1 - item // 2) * LANES
             out_ref[0, :, lanes(start)] = part[here, z, kept]
 
         @pl.when(jnp.logical_not(narrow))
         def _():
-            f_copy(item, x).start()
             out_ref[layer, :, lanes(own_half + chunk * LANES)] = part[here, z, kept]
 
         @pl.when(item + slots < items)
@@ -722,31 +762,35 @@
             def _():
                 signal(from_left, right)
 
-    for copy in loads[: 2 + NARROW]:
+    for unit in range(line - 1):
+        loads[unit].wait()
+        send(jnp.int32(unit))
+    for copy in loads[line - 1 : early_loads]:
         copy.wait()
-
-    @pl.loop(0, AHEAD_UNITS)
-    def _(unit):
-        send(unit)
-
-    for copy in loads[2 + NARROW :]:
-        copy.wait()
-
-    @pl.loop(0, items + line - 1)
+    for unit in range(line - 1, AHEAD_UNITS):
+        send(jnp.int32(unit))
+
+    @pl.loop(0, items + line)
     def _(step):
-        def guard(item, action):
-            pl.when(jnp.logical_and(item >= 0, item < items))(lambda: action(item))
+        def guard(turn, action):
+            item = turn - (turn > NARROW).astype(jnp.int32)
+            real = jnp.logical_and(turn >= 0, turn != NARROW)
+            pl.when(jnp.logical_and(real, item < items))(lambda: action(item))
 
         for stage in reversed(range(1, line - 1)):
             guard(step - stage, functools.partial(middle, stage=stage))
         guard(step, begin)
         guard(step - (line - 1), finish)
 
+        @pl.loop(exchanged(step - 1), exchanged(step))
+        def _(item):
+            exchange(item)
+
     @pl.loop(units - SEND_SLOTS, units)
     def _(unit):
         act_copy(unit, 0).wait_send()
 
-    @pl.loop(items - slots, items)
+    @pl.loop(0, items)
     def _(item):
         n_copy(item).wait_send()
 
@@ -830,20 +874,21 @@
             pltpu.VMEM((slots, line, 2 * rows, LANES), f32),
             pltpu.VMEM((slots, line + 1, 2 * rows, LANES), f32),
             pltpu.VMEM((NARROW, rows, LANES), f32),
+            pltpu.VMEM((items, rows, LANES), f32),
             pltpu.VMEM((8, LANES), f32),
             pltpu.VMEM((8, LANES), f32),
             pltpu.VMEM((col_count - 1, 8, LANES), f32),
             pltpu.VMEM((count - 1, 8, LANES), f32),
-            dma((NARROW + 3 * layers,)),
+            dma((NARROW + line + 3 * layers - 1,)),
             dma((SEND_SLOTS,)), dma((ACT_SLOTS,)), dma((line,)),
-            dma((line, col_count - 1)), dma((line, col_count - 1)),
+            dma((line, col_count - 1)), dma((line, col_count)),
             dma((slots, line)), dma((slots, line)), dma((slots, line)), dma((slots, line)),
-            dma((slots,)), dma((items,)),
+            dma((items,)), dma((items,)),
             dma((col_count - 1,)), dma((col_count - 1,)), dma((count - 1,)), dma((count - 1,)),
             regular((ACT_SLOTS,)), regular((line,)), regular, regular,
         ],
         compiler_params=pltpu.CompilerParams(
-            collective_id=0, has_side_effects=True, vmem_limit_bytes=62 * 2**20
+            collective_id=0, has_side_effects=True, vmem_limit_bytes=67043328
         ),
     )(cotangent, activations)
 
@@ -854,7 +899,7 @@
     rows = cotangent.shape[2] // count
     chunks = activations.shape[2] // (2 * LANES)
     aligned = activations.shape[1] % LANES == 0 and activations.shape[2] % (2 * LANES) == 0
-    return aligned and line >= 3 and 2 * rows == LANES * mesh_shape["col"] and chunks - NARROW // 2 > line
+    return aligned and line >= 3 and 2 * rows == LANES * mesh_shape["col"] and mesh_shape["col"] % 2 == 0 and chunks - NARROW // 2 > line
 
 
 def local(

time: 369 us -> 355 us (0.962)
  Pallas kernels: 334 us -> 318 us
    pallas_call x1, Pallas kernels: 334 us -> 318 us  [factor_gradient(): pl.pallas_call(functools.partial(factor_kernel, count, col_count), out_sh...]
where the time goes in v2:
time: 355 us
  Pallas kernels  318 us (90%)
  other arithmetic  23.2 us (7%)
  blocking collectives  10.4 us (3%)
    pallas_call x1, Pallas kernels, factor_gradient(): pl.pallas_call(functools.partial(factor_kernel, count, col_count), out_sh...  318 us
    pmax x1, blocking collectives, local(): moment_max, square_max = lax.pmax((moment_part, square_part), 'col')  10.4 us

profile of v2, /device:TPU:0, one launch (start us, length us, event | category | flops | bytes accessed | tf_op | source)
XLA Modules:
  0.0 354.6 jit_solution(12772404332123546553)
XLA Ops:
  0.7 0.0 copy-start.7
  0.7 0.5 copy-done.7
  1.2 1.4 fusion.28
  2.6 317.9 %shard_map.110 = (f32[2,256,2048]{2,1,0:T(8,128)}, f32[8,128]{1,0:T(8,128)}) custom-call(bf16[2,896,2048]{2,1,0:T(8,128)(2,1)} %cot_hbm.1, bf16[2,896,2048]{2,1,0:T(8,128)(2,1)} %act_hbm.1), custom_call_target="tpu_custom_call" | custom-call | tf_op jit(solution)/shard_map/pallas_call | solution.py:857
  320.5 1.3 reduce_sum.82
  322.5 0.0 copy-start.8
  322.5 0.0 copy-start.1
  322.5 0.0 copy-start.3
  322.5 0.0 copy-start.4
  322.5 5.5 %fusion.12 = (f32[256]{0:T(256)S(1)}, f32[256]{0:T(256)S(1)}, f32[256]{0:T(256)S(1)}, f32[256]{0:T(256)S(1)}) fusion(f32[2,256,2048]{2,1,0:T(8,128)} %get-tuple-element.8, f32[256]{0:T(256)} %get-tuple-element.15, f32[]{:T(128)S(6)} %min.3, bf16[2,256,2048]{2,1,0:T(8,128)(2,1)} %param.11, f32[256]{0:T(256)} %get-tuple-element.16, f32[256]{0:T(256)} %get-tuple-element.23, ...), kind=kLoop, calls=%fused_computation.25 | loop fusion | flops 15727616 | bytes 8396804 | tf_op jit(solution)/shard_map/reduce_max | solution.py:931
  328.0 0.0 copy-done.8
  328.0 0.1 broadcast_multiply_fusion
  328.1 10.4 %all-reduce = (f32[256,4]{0,1:T(4,128)S(1)}, f32[256,4]{0,1:T(4,128)S(1)}, f32[256,4]{0,1:T(4,128)S(1)}, f32[256,4]{0,1:T(4,128)S(1)}) all-reduce(f32[256,4]{0,1:T(4,128)S(1)} %get-tuple-element.37, f32[256,4]{0,1:T(4,128)S(1)} %get-tuple-element.36, f32[256,4]{0,1:T(4,128)S(1)} %get-tuple-element.38, ...), channel_id=1, replica_groups=mesh['dp'=8,'col'=4] {'col'}, use_global_device_ids=true, to_apply=%region_12.13 | all-reduce | flops 4096 | bytes 32768 | tf_op jit(solution)/shard_map/pmax | solution.py:938
  338.5 0.1 multiply_reduce_fusion.1
  338.6 0.6 pad_maximum_fusion.3
  339.3 0.0 copy-done.1
  339.3 0.0 copy-done.3
  339.3 0.0 copy-done.4
  339.3 0.0 copy-start
  339.3 0.0 copy-start.2
  339.3 0.0 copy-start.5
  339.3 0.0 copy-start.6
  339.3 2.7 divide_convert_fusion.1
  342.0 0.4 copy-done
  342.4 0.7 copy-done.2
  343.1 0.0 copy-done.5
  343.1 0.0 copy-done.6
  343.1 6.3 %multiply_subtract_fusion.1 = (f32[1,256,2048]{2,1,0:T(8,128)S(1)}, f32[1,256,2048]{2,1,0:T(8,128)S(1)}, bf16[1,256,2048]{2,1,0:T(8,128)(2,1)S(1)}, bf16[1,256,2048]{2,1,0:T(8,128)(2,1)S(1)}) fusion(f32[2,256,2048]{2,1,0:T(8,128)} %param.9, f32[2,256,2048]{2,1,0:T(8,128)S(1)} %copy-done, f32[]{:T(128)S(6)} %min.3, f32[256]{0:T(256)S(1)} %copy-done.4, ...), kind=kLoop, calls=%fused_computation.49 | loop fusion | flops 23068672 | bytes 18880516 | tf_op jit(solution)/shard_map/sub | solution.py:945
  349.4 2.3 pad_maximum_fusion
  351.6 1.5 pad_maximum_fusion.2
  353.1 1.5 pad_maximum_fusion.1
  (3 shorter events, 0.0 us)
Async XLA Ops:
  0.7 0.5 copy-start.7
  322.5 5.5 %copy-start.8 = (f32[4]{0:T(128)S(1)}, f32[4]{0:T(128)}, u32[]{:S(2)}) copy-start(f32[4]{0:T(128)} %copy-done.7) | copy-start | bytes 52
  322.5 16.8 %copy-start.1 = (bf16[2,256,2048]{2,1,0:T(8,128)(2,1)S(1)}, bf16[2,256,2048]{2,1,0:T(8,128)(2,1)}, u32[]{:S(2)}) copy-start(bf16[2,256,2048]{2,1,0:T(8,128)(2,1)} %param.10) | copy-start | bytes 6291460
  322.5 16.7 %copy-start.3 = (f32[256]{0:T(256)S(1)}, f32[256]{0:T(256)}, u32[]{:S(2)}) copy-start(f32[256]{0:T(256)} %get-tuple-element.15) | copy-start | bytes 3076
  322.5 16.7 %copy-start.4 = (f32[256]{0:T(256)S(1)}, f32[256]{0:T(256)}, u32[]{:S(2)}) copy-start(f32[256]{0:T(256)} %get-tuple-element.24) | copy-start | bytes 3076
  339.3 3.1 copy-start
  339.3 3.8 %copy-start.2 = (bf16[2,256,2048]{2,1,0:T(8,128)(2,1)S(1)}, bf16[2,256,2048]{2,1,0:T(8,128)(2,1)}, u32[]{:S(2)}) copy-start(bf16[2,256,2048]{2,1,0:T(8,128)(2,1)} %param.11) | copy-start | bytes 6291460
  339.3 3.8 %copy-start.5 = (f32[256]{0:T(256)S(1)}, f32[256]{0:T(256)}, u32[]{:S(2)}) copy-start(f32[256]{0:T(256)} %get-tuple-element.16) | copy-start | bytes 3076
  339.3 3.8 %copy-start.6 = (f32[256]{0:T(256)S(1)}, f32[256]{0:T(256)}, u32[]{:S(2)}) copy-start(f32[256]{0:T(256)} %get-tuple-element.23) | copy-start | bytes 3076

commit v3 on v2

--- a/solution.py
+++ b/solution.py
@@ -346,13 +346,17 @@
 ACT_SLOTS = 5
 NARROW = 2
 RELEASE = 3
+PEAK_ROWS = 32
+APPLY_ROWS = 64
 
 
 def factor_kernel(
-    count, col_count, cot_hbm, act_hbm, out_ref, sq_ref,
+    count, col_count, cot_hbm, act_hbm, weights_hbm, moments_hbm, squares_hbm, moment_scale, square_scale,
+    new_weights, new_moments, new_squares, new_moment_scale, new_square_scale, grad,
+    scale_rows, peak, peak_rows,
     cot_raw, act_raw, narrow_act, cot_t, act_cat, xs, xr, crx, part, arr, narrow_in, held,
     own_sq, sum_sq, col_sq, dp_sq,
-    ld_sem, xs_sem, xr_sem, pr_sem, cs_sem, cr_sem, rs_sem, rr_sem, ls_sem, ll_sem, fs_sem, fr_sem,
+    ld_sem, w_in, w_out, c_in, c_out, ms_sem, mr_sem, xs_sem, xr_sem, pr_sem, cs_sem, cr_sem, rs_sem, rr_sem, ls_sem, ll_sem, fs_sem, fr_sem,
     qs_sem, qr_sem, ds_sem, dr_sem, act_free, cot_free, from_right, from_left,
 ):
     layers, tokens, cols = act_hbm.shape
@@ -370,6 +374,8 @@
     units = first_units + (layers - 1) * layer_units
     all_sent = items - chunks + line - 2
     groups = col_count // 2
+    pieces = cols // LANES
+    features = cot_hbm.shape[2]
     me = lax.axis_index("dp")
     mine = lax.axis_index("col")
     z = me // 2
@@ -488,7 +494,7 @@
 
     def f_copy(item, side):
         layer, narrow, chunk = describe(item)
-        where = out_ref.at[layer, :, lanes(side * half + chunk * LANES)]
+        where = grad.at[layer, :, lanes(side * half + chunk * LANES)]
         return remote(held.at[item], where, fs_sem.at[item], fr_sem.at[item], peer)
 
     def exchange(item):
@@ -669,6 +675,41 @@
 
             l_copy(here, target).start()
 
+    def weight_place(layer, piece):
+        row = pl.ds(pl.multiple_of(layer * rows, 8), rows)
+        return crx.at[piece // col_count, piece % col_count, row]
+
+    def weight_in(layer, piece):
+        return pltpu.make_async_copy(
+            weights_hbm.at[layer, :, lanes(piece * LANES)], weight_place(layer, piece), w_in.at[layer, piece]
+        )
+
+    def weight_out(layer, piece):
+        return pltpu.make_async_copy(
+            weight_place(layer, piece), new_weights.at[layer, :, lanes(piece * LANES)], w_out.at[layer, piece]
+        )
+
+    def code_in(layer, kind):
+        source = (moments_hbm, squares_hbm)[kind].at[layer]
+        return pltpu.make_async_copy(
+            source, cot_raw.at[layer, pl.ds(kind * rows, rows), pl.ds(0, cols)], c_in.at[layer, kind]
+        )
+
+    def code_out(layer, piece, kind):
+        place = cot_raw.at[layer, pl.ds(kind * rows, rows), lanes(piece * LANES)]
+        target = (new_moments, new_squares)[kind].at[layer, :, lanes(piece * LANES)]
+        return pltpu.make_async_copy(place, target, c_out.at[layer, piece, kind])
+
+    def spread_scales():
+        for layer in range(layers):
+            for kind in range(2):
+                source = (moment_scale, square_scale)[kind]
+                factor = (beta_one, beta_two)[kind]
+                row = source[layer, pl.ds(mine, 1), :] * factor
+                for part_at in range(0, rows, LANES):
+                    tile = jnp.broadcast_to(row[:, part_at : part_at + LANES], (LANES, LANES))
+                    scale_rows[kind, layer, part_at : part_at + LANES] = tile.T
+
     def begin(item):
         layer, narrow, chunk = describe(item)
         ready(item, 0)
@@ -694,6 +735,17 @@
             for copy in loads[early_loads:]:
                 copy.wait()
 
+        @pl.when(item == items - 2)
+        def _():
+            spread_scales()
+            for index in range(layers):
+                for kind in range(2):
+                    code_in(index, kind).start()
+
+            @pl.loop(0, layers * pieces)
+            def _(index):
+                weight_in(index // pieces, index % pieces).start()
+
         @pl.when(jnp.logical_and(jnp.logical_not(narrow), chunk == 0))
         def _():
             for early in range(2, line - 1):
@@ -713,12 +765,28 @@
     def middle(item, stage):
         ready(item, stage)
         hop(item, stage)
+
+    def add_squares(value):
+        rows8 = value.reshape(value.shape[0] // 8, 8, LANES)
+        own_sq[...] += jnp.sum(rows8 * rows8, axis=0)
+
+    def join_narrow():
+        for item in range(NARROW):
+            n_copy(item).wait_recv()
+            where = lanes((item % 2) * half + (chunks - 1 - item // 2) * LANES)
+            value = grad[0, :, where] + narrow_in[item]
+            grad[0, :, where] = value
+            add_squares(value)
 
     def finish(item):
         layer, narrow, chunk = describe(item)
         here = item % slots
         ready(item, line - 1)
 
+        @pl.when(item == items - 2)
+        def _():
+            join_narrow()
+
         form(item, z)
 
         @pl.when(has_left)
@@ -746,11 +814,12 @@
         @pl.when(narrow)
         def _():
             start = (item % 2) * half + (chunks - 1 - item // 2) * LANES
-            out_ref[0, :, lanes(start)] = part[here, z, kept]
+            grad[0, :, lanes(start)] = part[here, z, kept]
 
         @pl.when(jnp.logical_not(narrow))
         def _():
-            out_ref[layer, :, lanes(own_half + chunk * LANES)] = part[here, z, kept]
+            grad[layer, :, lanes(own_half + chunk * LANES)] = part[here, z, kept]
+            add_squares(part[here, z])
 
         @pl.when(item + slots < items)
         def _():
@@ -762,6 +831,7 @@
             def _():
                 signal(from_left, right)
 
+    own_sq[...] = jnp.zeros_like(own_sq)
     for unit in range(line - 1):
         loads[unit].wait()
         send(jnp.int32(unit))
@@ -785,31 +855,6 @@
         @pl.loop(exchanged(step - 1), exchanged(step))
         def _(item):
             exchange(item)
-
-    @pl.loop(units - SEND_SLOTS, units)
-    def _(unit):
-        act_copy(unit, 0).wait_send()
-
-    @pl.loop(0, items)
-    def _(item):
-        n_copy(item).wait_send()
-
-    for item in range(NARROW):
-        n_copy(item).wait_recv()
-        start = (item % 2) * half + (chunks - 1 - item // 2) * LANES
-        out_ref[0, :, start : start + LANES] += narrow_in[item]
-
-    @pl.loop(NARROW, items)
-    def _(item):
-        f_copy(item, 1 - x).wait_recv()
-
-    def square_rows(index, total):
-        layer = index // (rows // 8)
-        at = pl.multiple_of(index % (rows // 8) * 8, 8)
-        for piece in range(cols // LANES):
-            value = out_ref[layer, pl.ds(at, 8), piece * LANES : (piece + 1) * LANES]
-            total = total + value * value
-        return total
 
     def spread(src, landing, send_sems, recv_sems, axis, index, size):
         copies = []
@@ -831,14 +876,124 @@
             total = total + landing[offset - 1]
         return total
 
-    own_sq[...] = lax.fori_loop(
-        0, layers * rows // 8, square_rows, jnp.zeros((8, LANES), jnp.float32)
-    )
     sum_sq[...] = spread(own_sq, col_sq, qs_sem, qr_sem, "col", mine, col_count)
-    sq_ref[...] = spread(sum_sq, dp_sq, ds_sem, dr_sem, "dp", me, count)
-
-
-def factor_gradient(activations, cotangent, mesh_shape):
+    total = spread(sum_sq, dp_sq, ds_sem, dr_sem, "dp", me, count)
+    total = jnp.sum(jnp.sum(total, axis=0, keepdims=True), axis=1, keepdims=True)
+    rms = jnp.sqrt(total / float(layers * features * cols * col_count) + norm_eps)
+    clip = jnp.minimum(1.0, 1.0 / rms)
+    moment_gain = clip * (1.0 - beta_one)
+    square_gain = clip * clip * (1.0 - beta_two)
+    correct_one = 1.0 - beta_one**STEP
+    correct_two = 1.0 - beta_two**STEP
+
+    for index in range(layers):
+        for kind in range(2):
+            code_in(index, kind).wait()
+
+    @pl.loop(NARROW, items)
+    def _(item):
+        f_copy(item, 1 - x).wait_recv()
+
+    def moments_of(layer, at, height, piece):
+        where = lanes(piece * LANES)
+        value = grad[layer, pl.ds(at, height), where]
+        moment = cot_raw[layer, pl.ds(at, height), where].astype(jnp.float32)
+        square = cot_raw[layer, pl.ds(pl.multiple_of(rows + at, 16), height), where].astype(jnp.float32)
+        moment = moment * scale_rows[0, layer, pl.ds(at, height)] + moment_gain * value
+        square = square * scale_rows[1, layer, pl.ds(at, height)] + square_gain * (value * value)
+        return moment, square
+
+    @pl.loop(0, layers * (rows // PEAK_ROWS))
+    def _(index):
+        layer = index // (rows // PEAK_ROWS)
+        at = pl.multiple_of(index % (rows // PEAK_ROWS) * PEAK_ROWS, PEAK_ROWS)
+        high_moment = jnp.zeros((PEAK_ROWS, LANES), jnp.float32)
+        high_square = jnp.zeros((PEAK_ROWS, LANES), jnp.float32)
+        for piece in range(pieces):
+            moment, square = moments_of(layer, at, PEAK_ROWS, piece)
+            high_moment = jnp.maximum(high_moment, jnp.abs(moment))
+            high_square = jnp.maximum(high_square, square)
+        peak[0, layer, pl.ds(at, PEAK_ROWS)] = high_moment
+        peak[1, layer, pl.ds(at, PEAK_ROWS)] = high_square
+
+    for layer in range(layers):
+        for kind in range(2):
+            for at in range(0, rows, LANES):
+                tile = peak[kind, layer, at : at + LANES].T
+                row = jnp.max(tile, axis=0, keepdims=True)
+                peak_rows[mine, kind, layer : layer + 1, at : at + LANES] = row
+                inverse = 1.0 / (row + scale_eps)
+                peak[kind, layer, at : at + LANES] = jnp.broadcast_to(inverse, (LANES, LANES)).T
+
+    def peak_copy(offset):
+        return pltpu.make_async_remote_copy(
+            src_ref=peak_rows.at[mine], dst_ref=peak_rows.at[mine],
+            send_sem=ms_sem.at[offset - 1], recv_sem=mr_sem.at[mine],
+            device_id={"col": lax.rem(mine + offset, col_count)},
+            device_id_type=pl.DeviceIdType.MESH,
+        )
+
+    def peak_arrival(owner):
+        return pltpu.make_async_remote_copy(
+            src_ref=peak_rows.at[owner], dst_ref=peak_rows.at[owner],
+            send_sem=ms_sem.at[0], recv_sem=mr_sem.at[owner],
+            device_id={"col": partner}, device_id_type=pl.DeviceIdType.MESH,
+        )
+
+    for offset in range(1, col_count):
+        peak_copy(offset).start()
+
+    @pl.loop(0, layers * pieces)
+    def _(index):
+        layer = index // pieces
+        piece = index % pieces
+        where = lanes(piece * LANES)
+        weight_in(layer, piece).wait()
+
+        for at in range(0, rows, APPLY_ROWS):
+            moment, square = moments_of(layer, at, APPLY_ROWS, piece)
+            span = pl.ds(at, APPLY_ROWS)
+            cot_raw[layer, span, where] = (moment * peak[0, layer, span]).astype(jnp.bfloat16)
+            cot_raw[layer, pl.ds(rows + at, APPLY_ROWS), where] = (square * peak[1, layer, span]).astype(jnp.bfloat16)
+            ratio = moment * (1.0 / correct_one) / (jnp.sqrt(square * (1.0 / correct_two)) + adam_eps)
+            place = (piece // col_count, piece % col_count, pl.ds(pl.multiple_of(layer * rows + at, 8), APPLY_ROWS))
+            weights = crx[place]
+            crx[place] = weights - learn_rate * (decay_rate * weights + ratio)
+
+        weight_out(layer, piece).start()
+        for kind in range(2):
+            code_out(layer, piece, kind).start()
+
+    for offset in range(1, col_count):
+        peak_arrival(lax.rem(mine + offset, col_count)).wait_recv()
+    for owner in range(col_count):
+        for layer in range(layers):
+            new_moment_scale[layer, owner : owner + 1, :] = peak_rows[owner, 0, layer : layer + 1, :]
+            new_square_scale[layer, owner : owner + 1, :] = peak_rows[owner, 1, layer : layer + 1, :]
+
+    for offset in range(1, col_count):
+        peak_copy(offset).wait_send()
+
+    @pl.loop(units - SEND_SLOTS, units)
+    def _(unit):
+        act_copy(unit, 0).wait_send()
+
+    @pl.loop(0, items)
+    def _(item):
+        n_copy(item).wait_send()
+
+    @pl.loop(0, layers * pieces)
+    def _(index):
+        layer = index // pieces
+        piece = index % pieces
+        weight_out(layer, piece).wait()
+        for kind in range(2):
+            code_out(layer, piece, kind).wait()
+
+
+def factor_step(
+    mesh_shape, activations, cotangent, master_weights, moment_codes, square_codes, moment_scales, square_scales
+):
     count = mesh_shape["dp"]
     col_count = mesh_shape["col"]
     layers, tokens, cols = activations.shape
@@ -847,6 +1002,7 @@
     rows = features // count
     half = cols // 2
     slots = line + 1
+    pieces = cols // LANES
     items = NARROW + layers * (half // LANES) - NARROW // 2
     piece = (tokens, LANES)
     f32, bf16 = jnp.float32, jnp.bfloat16
@@ -854,15 +1010,22 @@
     regular = pltpu.SemaphoreType.REGULAR
     vmem = pl.BlockSpec(memory_space=pltpu.VMEM)
     hbm = pl.BlockSpec(memory_space=pl.ANY)
-    return pl.pallas_call(
+    outs = pl.pallas_call(
         functools.partial(factor_kernel, count, col_count),
         out_shape=(
             jax.ShapeDtypeStruct((layers, rows, cols), f32),
-            jax.ShapeDtypeStruct((8, LANES), f32),
+            jax.ShapeDtypeStruct((layers, rows, cols), bf16),
+            jax.ShapeDtypeStruct((layers, rows, cols), bf16),
+            jax.ShapeDtypeStruct((layers, col_count, rows), f32),
+            jax.ShapeDtypeStruct((layers, col_count, rows), f32),
         ),
-        in_specs=[hbm, hbm],
-        out_specs=(vmem, vmem),
+        in_specs=[hbm, hbm, hbm, hbm, hbm, vmem, vmem],
+        out_specs=(hbm, hbm, hbm, vmem, vmem),
         scratch_shapes=[
+            pltpu.VMEM((layers, rows, cols), f32),
+            pltpu.VMEM((2, layers, rows, LANES), f32),
+            pltpu.VMEM((2, layers, rows, LANES), f32),
+            pltpu.VMEM((col_count, 2, layers, rows), f32),
             pltpu.VMEM((layers, tokens, features), bf16),
             pltpu.VMEM((layers, tokens, half), bf16),
             pltpu.VMEM((NARROW,) + piece, bf16),
@@ -880,6 +1043,8 @@
             pltpu.VMEM((col_count - 1, 8, LANES), f32),
             pltpu.VMEM((count - 1, 8, LANES), f32),
             dma((NARROW + line + 3 * layers - 1,)),
+            dma((layers, pieces)), dma((layers, pieces)), dma((layers, 2)), dma((layers, pieces, 2)),
+            dma((col_count - 1,)), dma((col_count,)),
             dma((SEND_SLOTS,)), dma((ACT_SLOTS,)), dma((line,)),
             dma((line, col_count - 1)), dma((line, col_count)),
             dma((slots, line)), dma((slots, line)), dma((slots, line)), dma((slots, line)),
@@ -890,16 +1055,23 @@
         compiler_params=pltpu.CompilerParams(
             collective_id=0, has_side_effects=True, vmem_limit_bytes=67043328
         ),
-    )(cotangent, activations)
-
-
-def fits_factors(activations, cotangent, mesh_shape):
+    )(
+        cotangent, activations, master_weights, moment_codes, square_codes,
+        moment_scales.transpose(0, 2, 1), square_scales.transpose(0, 2, 1),
+    )
+    return outs[:3] + (outs[3].transpose(0, 2, 1), outs[4].transpose(0, 2, 1))
+
+
+def fits_factors(activations, cotangent, block_count, mesh_shape):
     count = mesh_shape["dp"]
     line = count // 2
     rows = cotangent.shape[2] // count
     chunks = activations.shape[2] // (2 * LANES)
     aligned = activations.shape[1] % LANES == 0 and activations.shape[2] % (2 * LANES) == 0
-    return aligned and line >= 3 and 2 * rows == LANES * mesh_shape["col"] and mesh_shape["col"] % 2 == 0 and chunks - NARROW // 2 > line
+    layers, tokens, cols = activations.shape
+    aligned = aligned and rows % LANES == 0 and cols % LANES == 0 and block_count == mesh_shape["col"]
+    roomy = layers * rows <= tokens and cols <= cotangent.shape[2] and cols <= LANES * line * mesh_shape["col"]
+    return aligned and roomy and line >= 3 and 2 * rows == LANES * mesh_shape["col"] and mesh_shape["col"] % 2 == 0 and chunks - NARROW // 2 > line
 
 
 def local(
@@ -909,8 +1081,12 @@
     shard_rows = master_weights.shape[1]
     shard_cols = master_weights.shape[2]
     block_count = moment_scales.shape[2]
-    reduce = factor_gradient if fits_factors(activations, cotangent, mesh_shape) else reduced_gradient
-    gradient, squares = reduce(activations, cotangent, mesh_shape)
+    if fits_factors(activations, cotangent, block_count, mesh_shape):
+        return factor_step(
+            mesh_shape, activations, cotangent, master_weights, moment_codes, square_codes,
+            moment_scales, square_scales,
+        )
+    gradient, squares = reduced_gradient(activations, cotangent, mesh_shape)
     total_sq = jnp.sum(squares)
     rms = jnp.sqrt(total_sq / float(LAYERS * KV * D) + norm_eps)
     clip_factor = jnp.minimum(1.0, 1.0 / rms)

time: 355 us -> 334 us (0.941)
  other arithmetic: 23.2 us -> 0 us
  blocking collectives: 10.4 us -> 0 us
  local copies, waits for them, and re-layouts: 1.6 us -> 9.72 us
  Pallas kernels: 318 us -> 323 us
    pmax x1 -> x0, blocking collectives: 10.4 us -> none  [local(): moment_max, square_max = lax.pmax((moment_part, square_part), 'col')]
    unnamed x18 -> x13, local copies, waits for them, and re-layouts: 1.6 us -> 9.72 us
    sub x1 -> x0, other arithmetic: 6.27 us -> none  [local(): weights - learn_rate * (decay_rate * weights + ratio)]
    another operation x4 -> x0, other arithmetic: 5.89 us -> none  [the longest x1 2.28 us: local(): jnp.stack(outs_weights)]
    reduce_max x1 -> x0, other arithmetic: 5.49 us -> none  [local(): square_part = jnp.max(new_square, axis=1)[:, None] * selector]
    pallas_call x1, Pallas kernels: 318 us -> 323 us  [factor_step(): pl.pallas_call(functools.partial(factor_kernel, count, col_count), out_sh...]
where the time goes in v3:
time: 334 us
  Pallas kernels  323 us (97%)
  local copies, waits for them, and re-layouts  9.72 us (3%)
    pallas_call x1, Pallas kernels, factor_step(): pl.pallas_call(functools.partial(factor_kernel, count, col_count), out_sh...  323 us
    unnamed x13, local copies, waits for them, and re-layouts  9.72 us

profile of v3, /device:TPU:0, one launch (start us, length us, event | category | flops | bytes accessed | tf_op | source)
XLA Modules:
  0.0 333.6 jit_solution(15298537435997255766)
XLA Ops:
  0.6 323.2 %shard_map.110 = (f32[2,256,2048]{2,1,0:T(8,128)}, bf16[2,256,2048]{2,1,0:T(8,128)(2,1)}, bf16[2,256,2048]{2,1,0:T(8,128)(2,1)}, f32[2,4,256]{2,1,0:T(4,128)}, f32[2,4,256]{2,1,0:T(4,128)}) custom-call(bf16[2,896,2048]{2,1,0:T(8,128)(2,1)} %cot_hbm.1, bf16[2,896,2048]{2,1,0:T(8,128)(2,1)} %act_hbm.1, f32[2,256,2048]{2,1,0:T(8,128)} %weights_hbm.1, ...), custom_call_target="tpu_custom_call" | custom-call | tf_op jit(solution)/shard_map/pallas_call | solution.py:1013
  323.9 0.0 copy-start.1
  323.9 4.8 %copy.17 = f32[2,256,2048]{2,1,0:T(8,128)} copy(f32[2,256,2048]{2,1,0:T(8,128)} %get-tuple-element.20) | data formatting | bytes 8388608
  328.7 0.0 copy-done.1
  328.7 0.0 copy-start
  328.7 1.3 copy.18
  330.1 1.0 copy-done
  331.1 0.0 copy-start.3
  331.1 0.0 copy-start.2
  331.1 1.3 copy.19
  332.4 0.0 copy-done.3
  332.4 0.6 copy.20
  333.0 0.0 copy-done.2
  333.0 0.6 copy.21
Async XLA Ops:
  323.9 4.9 %copy-start.1 = (bf16[2,256,2048]{2,1,0:T(8,128)(2,1)S(1)}, bf16[2,256,2048]{2,1,0:T(8,128)(2,1)}, u32[]{:S(2)}) copy-start(bf16[2,256,2048]{2,1,0:T(8,128)(2,1)} %get-tuple-element.21) | copy-start | bytes 6291460
  328.7 2.3 copy-start
  331.1 1.3 copy-start.3
  331.1 1.9 copy-start.2

commit v4 on v3

--- a/solution.py
+++ b/solution.py
@@ -348,15 +348,17 @@
 RELEASE = 3
 PEAK_ROWS = 32
 APPLY_ROWS = 64
+STRIP_ROWS = 32
+APPLY_VMEM = 62 * 2**20
 
 
 def factor_kernel(
-    count, col_count, cot_hbm, act_hbm, weights_hbm, moments_hbm, squares_hbm, moment_scale, square_scale,
-    new_weights, new_moments, new_squares, new_moment_scale, new_square_scale, grad,
-    scale_rows, peak, peak_rows,
+    count, col_count, cot_hbm, act_hbm, moments_hbm, squares_hbm, moment_scale, square_scale,
+    grad_out, gain_out, new_moment_scale, new_square_scale, grad,
+    row_values, peak, peak_rows,
     cot_raw, act_raw, narrow_act, cot_t, act_cat, xs, xr, crx, part, arr, narrow_in, held,
     own_sq, sum_sq, col_sq, dp_sq,
-    ld_sem, w_in, w_out, c_in, c_out, ms_sem, mr_sem, xs_sem, xr_sem, pr_sem, cs_sem, cr_sem, rs_sem, rr_sem, ls_sem, ll_sem, fs_sem, fr_sem,
+    ld_sem, c_in, g_out, ms_sem, mr_sem, xs_sem, xr_sem, pr_sem, cs_sem, cr_sem, rs_sem, rr_sem, ls_sem, ll_sem, fs_sem, fr_sem,
     qs_sem, qr_sem, ds_sem, dr_sem, act_free, cot_free, from_right, from_left,
 ):
     layers, tokens, cols = act_hbm.shape
@@ -428,14 +430,23 @@
     early_loads = line + 1 + NARROW
 
     barrier = pltpu.get_barrier_semaphore()
-    for offset in range(1, count):
-        signal(barrier, lax.rem(me + offset, count))
+    signal(barrier, peer)
+
+    @pl.when(has_right)
+    def _():
+        signal(barrier, right)
+
+    @pl.when(has_left)
+    def _():
+        signal(barrier, left)
+
     for offset in range(1, col_count):
         pl.semaphore_signal(
             barrier, inc=1, device_id={"col": lax.rem(mine + offset, col_count)},
             device_id_type=pl.DeviceIdType.MESH,
         )
-    pl.semaphore_wait(barrier, count + col_count - 2)
+    sides = has_right.astype(jnp.int32) + has_left.astype(jnp.int32)
+    pl.semaphore_wait(barrier, col_count + sides)
 
     def remote(src, dst, send, recv, where):
         return pltpu.make_async_remote_copy(
@@ -675,30 +686,11 @@
 
             l_copy(here, target).start()
 
-    def weight_place(layer, piece):
-        row = pl.ds(pl.multiple_of(layer * rows, 8), rows)
-        return crx.at[piece // col_count, piece % col_count, row]
-
-    def weight_in(layer, piece):
-        return pltpu.make_async_copy(
-            weights_hbm.at[layer, :, lanes(piece * LANES)], weight_place(layer, piece), w_in.at[layer, piece]
-        )
-
-    def weight_out(layer, piece):
-        return pltpu.make_async_copy(
-            weight_place(layer, piece), new_weights.at[layer, :, lanes(piece * LANES)], w_out.at[layer, piece]
-        )
-
     def code_in(layer, kind):
         source = (moments_hbm, squares_hbm)[kind].at[layer]
         return pltpu.make_async_copy(
             source, cot_raw.at[layer, pl.ds(kind * rows, rows), pl.ds(0, cols)], c_in.at[layer, kind]
         )
-
-    def code_out(layer, piece, kind):
-        place = cot_raw.at[layer, pl.ds(kind * rows, rows), lanes(piece * LANES)]
-        target = (new_moments, new_squares)[kind].at[layer, :, lanes(piece * LANES)]
-        return pltpu.make_async_copy(place, target, c_out.at[layer, piece, kind])
 
     def spread_scales():
         for layer in range(layers):
@@ -708,7 +700,7 @@
                 row = source[layer, pl.ds(mine, 1), :] * factor
                 for part_at in range(0, rows, LANES):
                     tile = jnp.broadcast_to(row[:, part_at : part_at + LANES], (LANES, LANES))
-                    scale_rows[kind, layer, part_at : part_at + LANES] = tile.T
+                    row_values[kind, layer, part_at : part_at + LANES] = tile.T
 
     def begin(item):
         layer, narrow, chunk = describe(item)
@@ -741,10 +733,6 @@
             for index in range(layers):
                 for kind in range(2):
                     code_in(index, kind).start()
-
-            @pl.loop(0, layers * pieces)
-            def _(index):
-                weight_in(index // pieces, index % pieces).start()
 
         @pl.when(jnp.logical_and(jnp.logical_not(narrow), chunk == 0))
         def _():
@@ -883,8 +871,8 @@
     clip = jnp.minimum(1.0, 1.0 / rms)
     moment_gain = clip * (1.0 - beta_one)
     square_gain = clip * clip * (1.0 - beta_two)
-    correct_one = 1.0 - beta_one**STEP
-    correct_two = 1.0 - beta_two**STEP
+    gain_out[0] = jnp.broadcast_to(moment_gain, (8, LANES))
+    gain_out[1] = jnp.broadcast_to(square_gain, (8, LANES))
 
     for index in range(layers):
         for kind in range(2):
@@ -893,14 +881,17 @@
     @pl.loop(NARROW, items)
     def _(item):
         f_copy(item, 1 - x).wait_recv()
+
+    grad_copy = pltpu.make_async_copy(grad, grad_out, g_out)
+    grad_copy.start()
 
     def moments_of(layer, at, height, piece):
         where = lanes(piece * LANES)
         value = grad[layer, pl.ds(at, height), where]
         moment = cot_raw[layer, pl.ds(at, height), where].astype(jnp.float32)
         square = cot_raw[layer, pl.ds(pl.multiple_of(rows + at, 16), height), where].astype(jnp.float32)
-        moment = moment * scale_rows[0, layer, pl.ds(at, height)] + moment_gain * value
-        square = square * scale_rows[1, layer, pl.ds(at, height)] + square_gain * (value * value)
+        moment = moment * row_values[0, layer, pl.ds(at, height)] + moment_gain * value
+        square = square * row_values[1, layer, pl.ds(at, height)] + square_gain * (value * value)
         return moment, square
 
     @pl.loop(0, layers * (rows // PEAK_ROWS))
@@ -922,8 +913,6 @@
                 tile = peak[kind, layer, at : at + LANES].T
                 row = jnp.max(tile, axis=0, keepdims=True)
                 peak_rows[mine, kind, layer : layer + 1, at : at + LANES] = row
-                inverse = 1.0 / (row + scale_eps)
-                peak[kind, layer, at : at + LANES] = jnp.broadcast_to(inverse, (LANES, LANES)).T
 
     def peak_copy(offset):
         return pltpu.make_async_remote_copy(
@@ -943,27 +932,6 @@
     for offset in range(1, col_count):
         peak_copy(offset).start()
 
-    @pl.loop(0, layers * pieces)
-    def _(index):
-        layer = index // pieces
-        piece = index % pieces
-        where = lanes(piece * LANES)
-        weight_in(layer, piece).wait()
-
-        for at in range(0, rows, APPLY_ROWS):
-            moment, square = moments_of(layer, at, APPLY_ROWS, piece)
-            span = pl.ds(at, APPLY_ROWS)
-            cot_raw[layer, span, where] = (moment * peak[0, layer, span]).astype(jnp.bfloat16)
-            cot_raw[layer, pl.ds(rows + at, APPLY_ROWS), where] = (square * peak[1, layer, span]).astype(jnp.bfloat16)
-            ratio = moment * (1.0 / correct_one) / (jnp.sqrt(square * (1.0 / correct_two)) + adam_eps)
-            place = (piece // col_count, piece % col_count, pl.ds(pl.multiple_of(layer * rows + at, 8), APPLY_ROWS))
-            weights = crx[place]
-            crx[place] = weights - learn_rate * (decay_rate * weights + ratio)
-
-        weight_out(layer, piece).start()
-        for kind in range(2):
-            code_out(layer, piece, kind).start()
-
     for offset in range(1, col_count):
         peak_arrival(lax.rem(mine + offset, col_count)).wait_recv()
     for owner in range(col_count):
@@ -982,13 +950,95 @@
     def _(item):
         n_copy(item).wait_send()
 
-    @pl.loop(0, layers * pieces)
+    grad_copy.wait()
+
+
+def apply_kernel(
+    grad_hbm, weights_hbm, moments_hbm, squares_hbm, gain,
+    moment_scale, square_scale, moment_peak, square_peak,
+    new_weights, new_moments, new_squares, new_moment_scale, new_square_scale,
+    grad, row_values, weights, moments, squares, in_sem, out_sem,
+):
+    layers, rows, cols = grad.shape
+    blocks = rows // APPLY_ROWS
+    correct_one = 1.0 - beta_one**STEP
+    correct_two = 1.0 - beta_two**STEP
+
+    def block_of(index):
+        at = pl.multiple_of(index % blocks * APPLY_ROWS, APPLY_ROWS)
+        return index // blocks, pl.ds(at, APPLY_ROWS)
+
+    def arrivals(index):
+        layer, span = block_of(index)
+        sems = in_sem.at[index]
+        pairs = ((grad_hbm, grad), (moments_hbm, moments), (squares_hbm, squares), (weights_hbm, weights))
+        return [
+            pltpu.make_async_copy(src.at[layer, span], dst.at[layer, span], sems.at[number])
+            for number, (src, dst) in enumerate(pairs)
+        ]
+
+    def departures(index):
+        layer, span = block_of(index)
+        pairs = ((weights, new_weights), (moments, new_moments), (squares, new_squares))
+        return [
+            pltpu.make_async_copy(src.at[layer, span], dst.at[layer, span], out_sem.at[index, number])
+            for number, (src, dst) in enumerate(pairs)
+        ]
+
+    @pl.loop(0, layers * blocks)
     def _(index):
-        layer = index // pieces
-        piece = index % pieces
-        weight_out(layer, piece).wait()
-        for kind in range(2):
-            code_out(layer, piece, kind).wait()
+        for copy in arrivals(index):
+            copy.start()
+
+    new_moment_scale[...] = moment_peak[...]
+    new_square_scale[...] = square_peak[...]
+    mine = pl.ds(lax.axis_index("col"), 1)
+    for layer in range(layers):
+        lines = (
+            moment_scale[layer, mine] * beta_one,
+            square_scale[layer, mine] * beta_two,
+            1.0 / (moment_peak[layer, mine] + scale_eps),
+            1.0 / (square_peak[layer, mine] + scale_eps),
+        )
+        for kind, row in enumerate(lines):
+            for at in range(0, rows, LANES):
+                tile = jnp.broadcast_to(row[:, at : at + LANES], (LANES, LANES))
+                row_values[kind, layer, at : at + LANES] = tile.T
+
+    moment_gain = gain[0, 0:1, 0:1]
+    square_gain = gain[1, 0:1, 0:1]
+
+    @pl.loop(0, layers * blocks)
+    def _(index):
+        layer, span = block_of(index)
+        for copy in arrivals(index):
+            copy.wait()
+
+        @pl.loop(0, APPLY_ROWS // STRIP_ROWS)
+        def _(strip):
+            at = index % blocks * APPLY_ROWS + strip * STRIP_ROWS
+            span = pl.ds(pl.multiple_of(at, STRIP_ROWS), STRIP_ROWS)
+            for piece in range(cols // LANES):
+                where = pl.ds(piece * LANES, LANES)
+                value = grad[layer, span, where]
+                moment = moments[layer, span, where].astype(jnp.float32) * row_values[0, layer, span]
+                square = squares[layer, span, where].astype(jnp.float32) * row_values[1, layer, span]
+                moment = moment + moment_gain * value
+                square = square + square_gain * (value * value)
+                moments[layer, span, where] = (moment * row_values[2, layer, span]).astype(jnp.bfloat16)
+                squares[layer, span, where] = (square * row_values[3, layer, span]).astype(jnp.bfloat16)
+                level = square * (1.0 / correct_two)
+                ratio = moment * (1.0 / correct_one) * pl.reciprocal(level * lax.rsqrt(level) + adam_eps)
+                old = weights[layer, span, where]
+                weights[layer, span, where] = old - learn_rate * (decay_rate * old + ratio)
+
+        for copy in departures(index):
+            copy.start()
+
+    @pl.loop(0, layers * blocks)
+    def _(index):
+        for copy in departures(index):
+            copy.wait()
 
 
 def factor_step(
@@ -1002,25 +1052,27 @@
     rows = features // count
     half = cols // 2
     slots = line + 1
-    pieces = cols // LANES
+    blocks = layers * rows // APPLY_ROWS
+    scale_shape = jax.ShapeDtypeStruct((layers, col_count, rows), jnp.float32)
     items = NARROW + layers * (half // LANES) - NARROW // 2
     piece = (tokens, LANES)
     f32, bf16 = jnp.float32, jnp.bfloat16
+    moment_scales = moment_scales.transpose(0, 2, 1)
+    square_scales = square_scales.transpose(0, 2, 1)
     dma = pltpu.SemaphoreType.DMA
     regular = pltpu.SemaphoreType.REGULAR
     vmem = pl.BlockSpec(memory_space=pltpu.VMEM)
     hbm = pl.BlockSpec(memory_space=pl.ANY)
-    outs = pl.pallas_call(
+    gradient, gain, moment_peak, square_peak = pl.pallas_call(
         functools.partial(factor_kernel, count, col_count),
         out_shape=(
             jax.ShapeDtypeStruct((layers, rows, cols), f32),
-            jax.ShapeDtypeStruct((layers, rows, cols), bf16),
-            jax.ShapeDtypeStruct((layers, rows, cols), bf16),
-            jax.ShapeDtypeStruct((layers, col_count, rows), f32),
-            jax.ShapeDtypeStruct((layers, col_count, rows), f32),
+            jax.ShapeDtypeStruct((2, 8, LANES), f32),
+            scale_shape,
+            scale_shape,
         ),
-        in_specs=[hbm, hbm, hbm, hbm, hbm, vmem, vmem],
-        out_specs=(hbm, hbm, hbm, vmem, vmem),
+        in_specs=[hbm, hbm, hbm, hbm, vmem, vmem],
+        out_specs=(hbm, vmem, vmem, vmem),
         scratch_shapes=[
             pltpu.VMEM((layers, rows, cols), f32),
             pltpu.VMEM((2, layers, rows, LANES), f32),
@@ -1043,7 +1095,7 @@
             pltpu.VMEM((col_count - 1, 8, LANES), f32),
             pltpu.VMEM((count - 1, 8, LANES), f32),
             dma((NARROW + line + 3 * layers - 1,)),
-            dma((layers, pieces)), dma((layers, pieces)), dma((layers, 2)), dma((layers, pieces, 2)),
+            dma((layers, 2)), dma,
             dma((col_count - 1,)), dma((col_count,)),
             dma((SEND_SLOTS,)), dma((ACT_SLOTS,)), dma((line,)),
             dma((line, col_count - 1)), dma((line, col_count)),
@@ -1056,8 +1108,32 @@
             collective_id=0, has_side_effects=True, vmem_limit_bytes=67043328
         ),
     )(
-        cotangent, activations, master_weights, moment_codes, square_codes,
-        moment_scales.transpose(0, 2, 1), square_scales.transpose(0, 2, 1),
+        cotangent, activations, moment_codes, square_codes,
+        moment_scales, square_scales,
+    )
+    outs = pl.pallas_call(
+        apply_kernel,
+        out_shape=(
+            jax.ShapeDtypeStruct(master_weights.shape, f32),
+            jax.ShapeDtypeStruct(moment_codes.shape, bf16),
+            jax.ShapeDtypeStruct(square_codes.shape, bf16),
+            scale_shape,
+            scale_shape,
+        ),
+        in_specs=[hbm, hbm, hbm, hbm, vmem, vmem, vmem, vmem, vmem],
+        out_specs=(hbm, hbm, hbm, vmem, vmem),
+        scratch_shapes=[
+            pltpu.VMEM((layers, rows, cols), f32),
+            pltpu.VMEM((4, layers, rows, LANES), f32),
+            pltpu.VMEM((layers, rows, cols), f32),
+            pltpu.VMEM((layers, rows, cols), bf16),
+            pltpu.VMEM((layers, rows, cols), bf16),
+            dma((blocks, 4)), dma((blocks, 3)),
+        ],
+        compiler_params=pltpu.CompilerParams(vmem_limit_bytes=APPLY_VMEM),
+    )(
+        gradient, master_weights, moment_codes, square_codes, gain,
+        moment_scales, square_scales, moment_peak, square_peak,
     )
     return outs[:3] + (outs[3].transpose(0, 2, 1), outs[4].transpose(0, 2, 1))
 
@@ -1070,7 +1146,7 @@
     aligned = activations.shape[1] % LANES == 0 and activations.shape[2] % (2 * LANES) == 0
     layers, tokens, cols = activations.shape
     aligned = aligned and rows % LANES == 0 and cols % LANES == 0 and block_count == mesh_shape["col"]
-    roomy = layers * rows <= tokens and cols <= cotangent.shape[2] and cols <= LANES * line * mesh_shape["col"]
+    roomy = layers * rows <= tokens and cols <= cotangent.shape[2]
     return aligned and roomy and line >= 3 and 2 * rows == LANES * mesh_shape["col"] and mesh_shape["col"] % 2 == 0 and chunks - NARROW // 2 > line
 
 

time: 334 us -> 327 us (0.979)
  local copies, waits for them, and re-layouts: 9.72 us -> 0 us
    pallas_call x0 -> x1, Pallas kernels: none -> 9.78 us  [factor_step(): pl.pallas_call(apply_kernel, out_shape=(jax.ShapeDtypeStruct(master_weigh...]
    unnamed x13 -> x0, local copies, waits for them, and re-layouts: 9.72 us -> none
    pallas_call x1, Pallas kernels: 323 us -> 317 us  [factor_step(): pl.pallas_call(functools.partial(factor_kernel, count, col_count), out_sh...]
where the time goes in v4:
time: 327 us
  Pallas kernels  326 us (100%)
    pallas_call x1, Pallas kernels, factor_step(): pl.pallas_call(functools.partial(factor_kernel, count, col_count), out_sh...  317 us
    pallas_call x1, Pallas kernels, factor_step(): pl.pallas_call(apply_kernel, out_shape=(jax.ShapeDtypeStruct(master_weigh...  9.78 us

profile of v4, /device:TPU:0, one launch (start us, length us, event | category | flops | bytes accessed | tf_op | source)
XLA Modules:
  0.0 327.0 jit_solution(11271418953697871172)
XLA Ops:
  0.6 316.6 %shard_map.110 = (f32[2,256,2048]{2,1,0:T(8,128)}, f32[2,8,128]{2,1,0:T(8,128)}, f32[2,4,256]{2,1,0:T(4,128)}, f32[2,4,256]{2,1,0:T(4,128)}) custom-call(bf16[2,896,2048]{2,1,0:T(8,128)(2,1)} %cot_hbm.1, bf16[2,896,2048]{2,1,0:T(8,128)(2,1)} %act_hbm.1, bf16[2,256,2048]{2,1,0:T(8,128)(2,1)} %moments_hbm.3, bf16[2,256,2048]{2,1,0:T(8,128)(2,1)} %squares_hbm.3, ...), custom_call_target="tpu_custom_call" | custom-call | tf_op jit(solution)/shard_map/pallas_call | solution.py:1066
  317.2 9.8 %shard_map.111 = (f32[2,256,2048]{2,1,0:T(8,128)}, bf16[2,256,2048]{2,1,0:T(8,128)(2,1)}, bf16[2,256,2048]{2,1,0:T(8,128)(2,1)}, f32[2,4,256]{2,1,0:T(4,128)}, f32[2,4,256]{2,1,0:T(4,128)}) custom-call(f32[2,256,2048]{2,1,0:T(8,128)} %get-tuple-element.14.grad_hbm, f32[2,256,2048]{2,1,0:T(8,128)} %weights_hbm.1, bf16[2,256,2048]{2,1,0:T(8,128)(2,1)} %moments_hbm.3, ...), custom_call_target="tpu_custom_call" | custom-call | tf_op jit(solution)/shard_map/pallas_call | solution.py:1114

commit v5 on v4

--- a/solution.py
+++ b/solution.py
@@ -346,6 +346,7 @@
 ACT_SLOTS = 5
 NARROW = 2
 RELEASE = 3
+SPLITS = 2
 PEAK_ROWS = 32
 APPLY_ROWS = 64
 STRIP_ROWS = 32
@@ -473,14 +474,18 @@
         slot = number % ACT_SLOTS
         return remote(xs.at[here], xr.at[slot], xs_sem.at[here], xr_sem.at[slot], peer)
 
-    def cot_copy(unit, place):
+    def cot_copy(unit, place, split):
         here = unit % SEND_SLOTS
-        return remote(xs.at[here], crx.at[place, mine], xs_sem.at[here], pr_sem.at[place], peer)
-
-    def col_copy(place, owner, number, where):
+        span = pl.ds(split * (tokens // SPLITS), tokens // SPLITS)
+        return remote(
+            xs.at[here, span], crx.at[place, mine, span], xs_sem.at[here], pr_sem.at[place, split], peer
+        )
+
+    def col_copy(place, owner, number, where, split):
+        piece = crx.at[place, owner, pl.ds(split * (tokens // SPLITS), tokens // SPLITS)]
         return pltpu.make_async_remote_copy(
-            src_ref=crx.at[place, owner], dst_ref=crx.at[place, owner],
-            send_sem=cs_sem.at[place, number], recv_sem=cr_sem.at[place, owner],
+            src_ref=piece, dst_ref=piece,
+            send_sem=cs_sem.at[place, number, split], recv_sem=cr_sem.at[place, owner, split],
             device_id={"col": where}, device_id_type=pl.DeviceIdType.MESH,
         )
 
@@ -526,7 +531,8 @@
         def _():
             layer = jnp.where(unit < first_units, 0, 1 + (unit - first_units) // layer_units)
             index = unit - unit_base(layer)
-            is_cot = jnp.logical_or(index < line - 1, index == 2 * line - 2)
+            mixed = index < 2 * line - 1
+            is_cot = jnp.logical_and(mixed, index % 2 == 0)
             here = unit % SEND_SLOTS
 
             @pl.when(unit >= SEND_SLOTS)
@@ -535,7 +541,7 @@
 
             @pl.when(is_cot)
             def _():
-                place = jnp.minimum(index, line - 1)
+                place = index // 2
                 start = block_target(place) * pair_rows + mine * LANES
                 xs[here] = cot_raw[layer, :, lanes(start)].astype(jnp.float32)
 
@@ -543,11 +549,12 @@
                 def _():
                     pl.semaphore_wait(cot_free.at[place], 1)
 
-                cot_copy(unit, place).start()
+                for split in range(SPLITS):
+                    cot_copy(unit, place, split).start()
 
             @pl.when(jnp.logical_not(is_cot))
             def _():
-                chunk = jnp.where(index < 2 * line - 2, index - (line - 1), index - line)
+                chunk = jnp.where(mixed, index // 2, index - line)
                 number = act_number(layer, chunk)
                 xs[here] = act_raw[layer, :, lanes(chunk * LANES)].astype(jnp.float32)
 
@@ -558,16 +565,18 @@
                 act_copy(unit, number).start()
 
     def forward(layer, place):
-        cot_copy(0, place).wait_recv()
-        for index in range(1, groups):
-            col_copy(place, mine, index, far(index)).start()
-        col_copy(place, mine, 0, partner).start()
-        send(unit_base(layer) + jnp.where(place < line - 1, place, 2 * line - 2) + AHEAD_UNITS)
+        for split in range(SPLITS):
+            cot_copy(0, place, split).wait_recv()
+            for index in range(1, groups):
+                col_copy(place, mine, index, far(index), split).start()
+            col_copy(place, mine, 0, partner, split).start()
+        send(unit_base(layer) + 2 * place + AHEAD_UNITS)
 
     def relay(place):
-        for index in range(1, groups):
-            col_copy(place, far(index), groups - 1 + index, partner).wait_recv()
-            col_copy(place, far(index), groups - 1 + index, partner).start()
+        for split in range(SPLITS):
+            for index in range(1, groups):
+                col_copy(place, far(index), groups - 1 + index, partner, split).wait_recv()
+                col_copy(place, far(index), groups - 1 + index, partner, split).start()
 
     def prepare(layer, place):
         base = block_target(place) * pair_rows
@@ -584,9 +593,10 @@
             prepare(layer, place)
 
         base = block_target(place) * pair_rows
-        col_copy(place, partner, 0, partner).wait_recv()
-        for index in range(1, groups):
-            col_copy(place, lax.rem(partner + 2 * index, col_count), 0, partner).wait_recv()
+        for split in range(SPLITS):
+            col_copy(place, partner, 0, partner, split).wait_recv()
+            for index in range(1, groups):
+                col_copy(place, lax.rem(partner + 2 * index, col_count), 0, partner, split).wait_recv()
 
         @pl.loop(0, col_count)
         def _(owner):
@@ -594,7 +604,8 @@
             cot_t[layer, lanes(base + owner * LANES), pl.ds(tokens, tokens)] = source.T.astype(jnp.bfloat16)
 
         for number in range(col_count - 1):
-            col_copy(place, mine, number, partner).wait_send()
+            for split in range(SPLITS):
+                col_copy(place, mine, number, partner, split).wait_send()
 
         @pl.when(layer < layers - 1)
         def _():
@@ -610,7 +621,7 @@
         def _():
             signal(act_free.at[slot], peer)
 
-        index = jnp.where(chunk < line - 1, chunk + line - 1, chunk + line)
+        index = jnp.where(chunk < line - 1, 2 * chunk + 1, chunk + line)
         send(unit_base(layer) + index + AHEAD_UNITS)
 
     def form(item, target):
@@ -648,15 +659,9 @@
             if place == 0:
                 @pl.when(layer == 0)
                 def _():
-                    for early in range(2):
-                        forward(layer, early)
-
-                for early in range(2, line - 1):
-                    forward(layer, early)
-                for early in range(2):
-                    relay(early)
-            if place == line - 1:
-                relay(place)
+                    forward(layer, 0)
+
+            relay(place)
             absorb(layer, place)
 
     def hop(item, stage):
@@ -734,21 +739,15 @@
                 for kind in range(2):
                     code_in(index, kind).start()
 
-        @pl.when(jnp.logical_and(jnp.logical_not(narrow), chunk == 0))
-        def _():
-            for early in range(2, line - 1):
-                relay(early)
+        @pl.when(jnp.logical_and(jnp.logical_not(narrow), chunk < line - 1))
+        def _():
+            forward(layer, chunk + 1)
 
         next_layer, next_first = opens(item + 1)
 
         @pl.when(jnp.logical_and(next_first, jnp.logical_and(next_layer > 0, item + 1 < items)))
         def _():
-            for place in range(2):
-                forward(next_layer, place)
-
-        @pl.when(jnp.logical_and(jnp.logical_not(narrow), chunk == line - 2))
-        def _():
-            forward(layer, line - 1)
+            forward(next_layer, 0)
 
     def middle(item, stage):
         ready(item, stage)
@@ -820,12 +819,11 @@
                 signal(from_left, right)
 
     own_sq[...] = jnp.zeros_like(own_sq)
-    for unit in range(line - 1):
-        loads[unit].wait()
-        send(jnp.int32(unit))
-    for copy in loads[line - 1 : early_loads]:
+    loads[0].wait()
+    send(jnp.int32(0))
+    for copy in loads[1:early_loads]:
         copy.wait()
-    for unit in range(line - 1, AHEAD_UNITS):
+    for unit in range(1, AHEAD_UNITS):
         send(jnp.int32(unit))
 
     @pl.loop(0, items + line)
@@ -835,7 +833,7 @@
             real = jnp.logical_and(turn >= 0, turn != NARROW)
             pl.when(jnp.logical_and(real, item < items))(lambda: action(item))
 
-        for stage in reversed(range(1, line - 1)):
+        for stage in range(1, line - 1):
             guard(step - stage, functools.partial(middle, stage=stage))
         guard(step, begin)
         guard(step - (line - 1), finish)
@@ -1097,8 +1095,8 @@
             dma((NARROW + line + 3 * layers - 1,)),
             dma((layers, 2)), dma,
             dma((col_count - 1,)), dma((col_count,)),
-            dma((SEND_SLOTS,)), dma((ACT_SLOTS,)), dma((line,)),
-            dma((line, col_count - 1)), dma((line, col_count)),
+            dma((SEND_SLOTS,)), dma((ACT_SLOTS,)), dma((line, SPLITS)),
+            dma((line, col_count - 1, SPLITS)), dma((line, col_count, SPLITS)),
             dma((slots, line)), dma((slots, line)), dma((slots, line)), dma((slots, line)),
             dma((items,)), dma((items,)),
             dma((col_count - 1,)), dma((col_count - 1,)), dma((count - 1,)), dma((count - 1,)),
@@ -1147,7 +1145,7 @@
     layers, tokens, cols = activations.shape
     aligned = aligned and rows % LANES == 0 and cols % LANES == 0 and block_count == mesh_shape["col"]
     roomy = layers * rows <= tokens and cols <= cotangent.shape[2]
-    return aligned and roomy and line >= 3 and 2 * rows == LANES * mesh_shape["col"] and mesh_shape["col"] % 2 == 0 and chunks - NARROW // 2 > line
+    return aligned and roomy and line >= 3 and 2 * rows == LANES * mesh_shape["col"] and mesh_shape["col"] % 2 == 0 and activations.shape[1] % (8 * SPLITS) == 0 and chunks - NARROW // 2 > line
 
 
 def local(

time: 327 us -> 323 us (0.988)
  Pallas kernels: 326 us -> 322 us
    pallas_call x1, Pallas kernels: 317 us -> 312 us  [factor_step(): pl.pallas_call(functools.partial(factor_kernel, count, col_count), out_sh...]
where the time goes in v5:
time: 323 us
  Pallas kernels  322 us (100%)
    pallas_call x1, Pallas kernels, factor_step(): pl.pallas_call(functools.partial(factor_kernel, count, col_count), out_sh...  312 us
    pallas_call x1, Pallas kernels, factor_step(): pl.pallas_call(apply_kernel, out_shape=(jax.ShapeDtypeStruct(master_weigh...  9.78 us

profile of v5, /device:TPU:0, one launch (start us, length us, event | category | flops | bytes accessed | tf_op | source)
XLA Modules:
  0.0 322.5 jit_solution(15184517910173627727)
XLA Ops:
  0.6 312.1 %shard_map.110 = (f32[2,256,2048]{2,1,0:T(8,128)}, f32[2,8,128]{2,1,0:T(8,128)}, f32[2,4,256]{2,1,0:T(4,128)}, f32[2,4,256]{2,1,0:T(4,128)}) custom-call(bf16[2,896,2048]{2,1,0:T(8,128)(2,1)} %cot_hbm.1, bf16[2,896,2048]{2,1,0:T(8,128)(2,1)} %act_hbm.1, bf16[2,256,2048]{2,1,0:T(8,128)(2,1)} %moments_hbm.3, bf16[2,256,2048]{2,1,0:T(8,128)(2,1)} %squares_hbm.3, ...), custom_call_target="tpu_custom_call" | custom-call | tf_op jit(solution)/shard_map/pallas_call | solution.py:1064
  312.8 9.8 %shard_map.111 = (f32[2,256,2048]{2,1,0:T(8,128)}, bf16[2,256,2048]{2,1,0:T(8,128)(2,1)}, bf16[2,256,2048]{2,1,0:T(8,128)(2,1)}, f32[2,4,256]{2,1,0:T(4,128)}, f32[2,4,256]{2,1,0:T(4,128)}) custom-call(f32[2,256,2048]{2,1,0:T(8,128)} %get-tuple-element.14.grad_hbm, f32[2,256,2048]{2,1,0:T(8,128)} %weights_hbm.1, bf16[2,256,2048]{2,1,0:T(8,128)(2,1)} %moments_hbm.3, ...), custom_call_target="tpu_custom_call" | custom-call | tf_op jit(solution)/shard_map/pallas_call | solution.py:1112

commit v6 on v5

--- a/solution.py
+++ b/solution.py
@@ -356,7 +356,7 @@
 def factor_kernel(
     count, col_count, cot_hbm, act_hbm, moments_hbm, squares_hbm, moment_scale, square_scale,
     grad_out, gain_out, new_moment_scale, new_square_scale, grad,
-    row_values, peak, peak_rows,
+    scales, row_values, peak, peak_rows,
     cot_raw, act_raw, narrow_act, cot_t, act_cat, xs, xr, crx, part, arr, narrow_in, held,
     own_sq, sum_sq, col_sq, dp_sq,
     ld_sem, c_in, g_out, ms_sem, mr_sem, xs_sem, xr_sem, pr_sem, cs_sem, cr_sem, rs_sem, rr_sem, ls_sem, ll_sem, fs_sem, fr_sem,
@@ -427,6 +427,8 @@
             load(cot_hbm.at[layer], cot_raw.at[layer])
             load(act_hbm.at[layer, :, pl.ds(peer_half, half)], act_raw.at[layer])
         load(act_hbm.at[layer, :, pl.ds(own_half, half)], act_cat.at[layer, pl.ds(0, tokens)])
+    load(moment_scale, scales.at[0])
+    load(square_scale, scales.at[1])
 
     early_loads = line + 1 + NARROW
 
@@ -700,9 +702,8 @@
     def spread_scales():
         for layer in range(layers):
             for kind in range(2):
-                source = (moment_scale, square_scale)[kind]
                 factor = (beta_one, beta_two)[kind]
-                row = source[layer, pl.ds(mine, 1), :] * factor
+                row = scales[kind, layer, pl.ds(mine, 1), :] * factor
                 for part_at in range(0, rows, LANES):
                     tile = jnp.broadcast_to(row[:, part_at : part_at + LANES], (LANES, LANES))
                     row_values[kind, layer, part_at : part_at + LANES] = tile.T
@@ -952,10 +953,11 @@
 
 
 def apply_kernel(
-    grad_hbm, weights_hbm, moments_hbm, squares_hbm, gain,
-    moment_scale, square_scale, moment_peak, square_peak,
+    grad_hbm, weights_hbm, moments_hbm, squares_hbm, gain_hbm,
+    moment_scale_hbm, square_scale_hbm, moment_peak_hbm, square_peak_hbm,
     new_weights, new_moments, new_squares, new_moment_scale, new_square_scale,
-    grad, row_values, weights, moments, squares, in_sem, out_sem,
+    gain, moment_scale, square_scale, moment_peak, square_peak,
+    grad, row_values, weights, moments, squares, in_sem, out_sem, small_in, small_out,
 ):
     layers, rows, cols = grad.shape
     blocks = rows // APPLY_ROWS
@@ -983,13 +985,29 @@
             for number, (src, dst) in enumerate(pairs)
         ]
 
+    small = [
+        pltpu.make_async_copy(src, dst, small_in.at[number])
+        for number, (src, dst) in enumerate((
+            (gain_hbm, gain), (moment_scale_hbm, moment_scale), (square_scale_hbm, square_scale),
+            (moment_peak_hbm, moment_peak), (square_peak_hbm, square_peak),
+        ))
+    ]
+    results = [
+        pltpu.make_async_copy(moment_peak, new_moment_scale, small_out.at[0]),
+        pltpu.make_async_copy(square_peak, new_square_scale, small_out.at[1]),
+    ]
+    for copy in small:
+        copy.start()
+
     @pl.loop(0, layers * blocks)
     def _(index):
         for copy in arrivals(index):
             copy.start()
 
-    new_moment_scale[...] = moment_peak[...]
-    new_square_scale[...] = square_peak[...]
+    for copy in small:
+        copy.wait()
+    for copy in results:
+        copy.start()
     mine = pl.ds(lax.axis_index("col"), 1)
     for layer in range(layers):
         lines = (
@@ -1037,6 +1055,9 @@
     def _(index):
         for copy in departures(index):
             copy.wait()
+
+    for copy in results:
+        copy.wait()
 
 
 def factor_step(
@@ -1069,10 +1090,11 @@
             scale_shape,
             scale_shape,
         ),
-        in_specs=[hbm, hbm, hbm, hbm, vmem, vmem],
+        in_specs=[hbm] * 6,
         out_specs=(hbm, vmem, vmem, vmem),
         scratch_shapes=[
             pltpu.VMEM((layers, rows, cols), f32),
+            pltpu.VMEM((2, layers, col_count, rows), f32),
             pltpu.VMEM((2, layers, rows, LANES), f32),
             pltpu.VMEM((2, layers, rows, LANES), f32),
             pltpu.VMEM((col_count, 2, layers, rows), f32),
@@ -1092,7 +1114,7 @@
             pltpu.VMEM((8, LANES), f32),
             pltpu.VMEM((col_count - 1, 8, LANES), f32),
             pltpu.VMEM((count - 1, 8, LANES), f32),
-            dma((NARROW + line + 3 * layers - 1,)),
+            dma((NARROW + line + 3 * layers + 1,)),
             dma((layers, 2)), dma,
             dma((col_count - 1,)), dma((col_count,)),
             dma((SEND_SLOTS,)), dma((ACT_SLOTS,)), dma((line, SPLITS)),
@@ -1118,15 +1140,20 @@
             scale_shape,
             scale_shape,
         ),
-        in_specs=[hbm, hbm, hbm, hbm, vmem, vmem, vmem, vmem, vmem],
-        out_specs=(hbm, hbm, hbm, vmem, vmem),
+        in_specs=[hbm] * 9,
+        out_specs=(hbm,) * 5,
         scratch_shapes=[
+            pltpu.VMEM((2, 8, LANES), f32),
+            pltpu.VMEM(scale_shape.shape, f32),
+            pltpu.VMEM(scale_shape.shape, f32),
+            pltpu.VMEM(scale_shape.shape, f32),
+            pltpu.VMEM(scale_shape.shape, f32),
             pltpu.VMEM((layers, rows, cols), f32),
             pltpu.VMEM((4, layers, rows, LANES), f32),
             pltpu.VMEM((layers, rows, cols), f32),
             pltpu.VMEM((layers, rows, cols), bf16),
             pltpu.VMEM((layers, rows, cols), bf16),
-            dma((blocks, 4)), dma((blocks, 3)),
+            dma((blocks, 4)), dma((blocks, 3)), dma((5,)), dma((2,)),
         ],
         compiler_params=pltpu.CompilerParams(vmem_limit_bytes=APPLY_VMEM),
     )(

time: 323 us -> 321 us (level)
  no operation moved by 1% of the time
where the time goes in v6:
time: 321 us
  Pallas kernels  320 us (100%)
    pallas_call x1, Pallas kernels, factor_step(): pl.pallas_call(functools.partial(factor_kernel, count, col_count), out_sh...  312 us
    pallas_call x1, Pallas kernels, factor_step(): pl.pallas_call(apply_kernel, out_shape=(jax.ShapeDtypeStruct(master_weigh...  8.57 us

profile of v6, /device:TPU:0, one launch (start us, length us, event | category | flops | bytes accessed | tf_op | source)
XLA Modules:
  0.0 320.7 jit_solution(1763402556685491862)
XLA Ops:
  0.6 311.5 %shard_map.110 = (f32[2,256,2048]{2,1,0:T(8,128)}, f32[2,8,128]{2,1,0:T(8,128)}, f32[2,4,256]{2,1,0:T(4,128)}, f32[2,4,256]{2,1,0:T(4,128)}) custom-call(bf16[2,896,2048]{2,1,0:T(8,128)(2,1)} %cot_hbm.1, bf16[2,896,2048]{2,1,0:T(8,128)(2,1)} %act_hbm.1, bf16[2,256,2048]{2,1,0:T(8,128)(2,1)} %moments_hbm.3, bf16[2,256,2048]{2,1,0:T(8,128)(2,1)} %squares_hbm.3, ...), custom_call_target="tpu_custom_call" | custom-call | tf_op jit(solution)/shard_map/pallas_call | solution.py:1085
  312.2 8.6 %shard_map.111 = (f32[2,256,2048]{2,1,0:T(8,128)}, bf16[2,256,2048]{2,1,0:T(8,128)(2,1)}, bf16[2,256,2048]{2,1,0:T(8,128)(2,1)}, f32[2,4,256]{2,1,0:T(4,128)}, f32[2,4,256]{2,1,0:T(4,128)}) custom-call(f32[2,256,2048]{2,1,0:T(8,128)} %get-tuple-element.14.grad_hbm, f32[2,256,2048]{2,1,0:T(8,128)} %weights_hbm.1, bf16[2,256,2048]{2,1,0:T(8,128)(2,1)} %moments_hbm.3, ...), custom_call_target="tpu_custom_call" | custom-call | tf_op jit(solution)/shard_map/pallas_call | solution.py:1134
